TPU v7x, 16 devices: a whole 2x2x2 slice. The times are simulated.
16 devices in a mesh: pp: 2 (over z), ep: 8 (over y, x, core).
Axes of the slice: x: 2, y: 2, z: 2, core: 2. Of those that a mesh axis runs over, the one named last changes fastest.
Arguments:
- x_fwd: bfloat16 [2, 6144, 256], P('pp', 'ep')
- x_bwd: bfloat16 [2, 6144, 256], P('pp', 'ep')
- grad_in: bfloat16 [2, 6144, 256], P('pp', 'ep')
- dense_in: bfloat16 [2, 2, 256, 1024], P('pp')
- dense_out: bfloat16 [2, 2, 1024, 256], P('pp')
- exp_gate: bfloat16 [2, 2, 384, 256, 128], P('pp', None, 'ep')
- exp_up: bfloat16 [2, 2, 384, 256, 128], P('pp', None, 'ep')
- exp_down: bfloat16 [2, 2, 384, 128, 256], P('pp', None, 'ep')
- route_fwd: int32 [2, 2, 6144, 8], P('pp', None, 'ep')
- gate_fwd: bfloat16 [2, 2, 6144, 8], P('pp', None, 'ep')
- route_bwd: int32 [2, 2, 6144, 8], P('pp', None, 'ep')
- gate_bwd: bfloat16 [2, 2, 6144, 8], P('pp', None, 'ep')
Outputs:
- output 1: bfloat16 [2, 6144, 256], P('pp', 'ep')
- output 2: bfloat16 [2, 6144, 256], P('pp', 'ep')
- output 3: float32 [2, 2, 384, 256, 128], P('pp', None, 'ep')
- output 4: float32 [2, 2, 384, 256, 128], P('pp', None, 'ep')
- output 5: float32 [2, 2, 384, 128, 256], P('pp', None, 'ep')
All inputs are finite; a program needn't handle non-finite values.
Results may differ from a plain program's by a relative error of at most 0.02.
Values are sent between devices in bfloat16 or wider.
A program may use at most 1 GiB of HBM per device.

v0:
```python
import jax
import jax.numpy as jnp
from jax import lax
from jax.sharding import PartitionSpec as P

NORM_EPS = 1e-6
CAP_FACTOR = 2


def rms_norm(values):
    return values * lax.rsqrt(jnp.mean(values * values, axis=-1, keepdims=True) + NORM_EPS)


def rms_back(values, grad_out):
    inv_rms = lax.rsqrt(jnp.mean(values * values, axis=-1, keepdims=True) + NORM_EPS)
    proj_mean = jnp.mean(grad_out * values, axis=-1, keepdims=True)
    return inv_rms * grad_out - values * (inv_rms * inv_rms * inv_rms) * proj_mean


def silu_grad(pre_act):
    sig_value = jax.nn.sigmoid(pre_act)
    return sig_value * (1.0 + pre_act * (1.0 - sig_value))


def dense_forward(tokens, w_in, w_out):
    normed = rms_norm(tokens.astype(jnp.float32)).astype(jnp.bfloat16)
    pre_act = jnp.dot(normed, w_in, preferred_element_type=jnp.float32)
    mid_act = jax.nn.silu(pre_act).astype(jnp.bfloat16)
    hidden = (tokens.astype(jnp.float32) + jnp.dot(mid_act, w_out, preferred_element_type=jnp.float32)).astype(jnp.bfloat16)
    return pre_act, hidden


def dense_backward(grad_hidden, tokens, pre_act, w_in, w_out):
    grad_dense = jnp.einsum('td,fd->tf', grad_hidden.astype(jnp.bfloat16), w_out, preferred_element_type=jnp.float32)
    grad_pre = (grad_dense * silu_grad(pre_act)).astype(jnp.bfloat16)
    grad_act = jnp.einsum('tf,df->td', grad_pre, w_in, preferred_element_type=jnp.float32)
    return (grad_hidden + rms_back(tokens.astype(jnp.float32), grad_act)).astype(jnp.bfloat16)


def expert_front(received, w_gate, w_up):
    gate_pre = jnp.einsum('secd,edf->secf', received, w_gate, preferred_element_type=jnp.float32)
    up_pre = jnp.einsum('secd,edf->secf', received, w_up, preferred_element_type=jnp.float32)
    expert_mid = (jax.nn.silu(gate_pre) * up_pre).astype(jnp.bfloat16)
    return gate_pre, up_pre, expert_mid


def expert_backward(received, grad_recv, gate_pre, up_pre, expert_mid, w_gate, w_up, w_down):
    grad_mid = jnp.einsum('secd,efd->secf', grad_recv, w_down, preferred_element_type=jnp.float32)
    grad_gate_pre = (grad_mid * up_pre * silu_grad(gate_pre)).astype(jnp.bfloat16)
    grad_up_pre = (grad_mid * jax.nn.silu(gate_pre)).astype(jnp.bfloat16)
    dw_down = jnp.einsum('secf,secd->efd', expert_mid, grad_recv, preferred_element_type=jnp.float32)
    dw_gate = jnp.einsum('secd,secf->edf', received, grad_gate_pre, preferred_element_type=jnp.float32)
    dw_up = jnp.einsum('secd,secf->edf', received, grad_up_pre, preferred_element_type=jnp.float32)
    grad_rows = (jnp.einsum('secf,edf->secd', grad_gate_pre, w_gate, preferred_element_type=jnp.float32) + jnp.einsum('secf,edf->secd', grad_up_pre, w_up, preferred_element_type=jnp.float32)).astype(jnp.bfloat16)
    return grad_rows, dw_gate, dw_up, dw_down


def solution(mesh):
    groups = mesh.shape['ep']
    stages = mesh.shape['pp']
    to_next = [(sender, (sender + 1) % stages) for sender in range(stages)]
    to_prev = [(sender, (sender - 1) % stages) for sender in range(stages)]

    def local_step(x_fwd, x_bwd, grad_in, dense_in, dense_out, exp_gate, exp_up, exp_down, route_fwd, gate_fwd, route_bwd, gate_bwd):
        n_tok, width = x_fwd.shape[1], x_fwd.shape[2]
        choices = route_fwd.shape[3]
        local_experts = exp_gate.shape[2]
        capacity = CAP_FACTOR * n_tok * choices // (local_experts * groups)
        slots_dev = local_experts * capacity

        def dispatch(rows, route):
            send_buf = jnp.zeros((groups * slots_dev, width), rows.dtype).at[route.reshape(-1)].set(rows.reshape(-1, width), unique_indices=True)
            received = lax.all_to_all(send_buf.reshape(groups, slots_dev, width), 'ep', 0, 0, tiled=True)
            return received.reshape(groups, local_experts, capacity, width)

        def combine(rows, route):
            returned = lax.all_to_all(rows.reshape(groups, slots_dev, width), 'ep', 0, 0, tiled=True)
            return returned.reshape(groups * slots_dev, width)[route]

        def block_front(tokens, route, weights):
            pre_act, hidden = dense_forward(tokens, weights[0], weights[1])
            normed = rms_norm(hidden.astype(jnp.float32)).astype(jnp.bfloat16)
            spread = jnp.broadcast_to(normed[:, None, :], (n_tok, choices, width))
            received = dispatch(spread, route)
            gate_pre, up_pre, expert_mid = expert_front(received, weights[2], weights[3])
            return tokens, pre_act, hidden, received, gate_pre, up_pre, expert_mid

        def block_finish(saved, route, gate, weights):
            expert_out = jnp.einsum('secf,efd->secd', saved[6], weights[4], preferred_element_type=jnp.float32).astype(jnp.bfloat16)
            picked = combine(expert_out, route)
            mixed = jnp.einsum('tk,tkd->td', gate, picked, preferred_element_type=jnp.float32)
            return (saved[2].astype(jnp.float32) + mixed).astype(jnp.bfloat16)

        def block_backward(grad_out, saved, route, gate, weights):
            tokens, pre_act, hidden, received, gate_pre, up_pre, expert_mid = saved
            grad_send = (gate.astype(jnp.float32)[:, :, None] * grad_out.astype(jnp.float32)[:, None, :]).astype(jnp.bfloat16)
            grad_recv = dispatch(grad_send, route)
            grad_rows, dw_gate, dw_up, dw_down = expert_backward(received, grad_recv, gate_pre, up_pre, expert_mid, weights[2], weights[3], weights[4])
            grad_norm = jnp.sum(combine(grad_rows, route), axis=1, dtype=jnp.float32)
            grad_hidden = grad_out.astype(jnp.float32) + rms_back(hidden.astype(jnp.float32), grad_norm)
            grad_tokens = dense_backward(grad_hidden, tokens, pre_act, weights[0], weights[1])
            return grad_tokens, dw_gate, dw_up, dw_down

        weights = [(dense_in[0, block], dense_out[0, block], exp_gate[0, block], exp_up[0, block], exp_down[0, block]) for block in range(2)]
        fwd_tokens = x_fwd[0]
        for block in range(2):
            saved = block_front(fwd_tokens, route_fwd[0, block], weights[block])
            fwd_tokens = block_finish(saved, route_fwd[0, block], gate_fwd[0, block], weights[block])
        saved_first = block_front(x_bwd[0], route_bwd[0, 0], weights[0])
        mid_tokens = block_finish(saved_first, route_bwd[0, 0], gate_bwd[0, 0], weights[0])
        saved_second = block_front(mid_tokens, route_bwd[0, 1], weights[1])
        grad_mid, wg_two, wu_two, wd_two = block_backward(grad_in[0], saved_second, route_bwd[0, 1], gate_bwd[0, 1], weights[1])
        grad_first, wg_one, wu_one, wd_one = block_backward(grad_mid, saved_first, route_bwd[0, 0], gate_bwd[0, 0], weights[0])
        y_next = lax.ppermute(fwd_tokens, 'pp', to_next)
        dx_prev = lax.ppermute(grad_first, 'pp', to_prev)
        return (y_next[None], dx_prev[None], jnp.stack([wg_one, wg_two])[None], jnp.stack([wu_one, wu_two])[None], jnp.stack([wd_one, wd_two])[None])

    tok_spec = P('pp', 'ep', None)
    dense_spec = P('pp', None, None, None)
    exp_spec = P('pp', None, 'ep', None, None)
    route_spec = P('pp', None, 'ep', None)
    return jax.shard_map(local_step, mesh=mesh, in_specs=(tok_spec, tok_spec, tok_spec, dense_spec, dense_spec, exp_spec, exp_spec, exp_spec, route_spec, route_spec, route_spec, route_spec), out_specs=(tok_spec, tok_spec, exp_spec, exp_spec, exp_spec), check_vma=False)
```

profile of v0, /device:TPU:0, one launch (start us, length us, event | category | flops | bytes accessed | tf_op | source)
XLA Modules:
  0.0 946.0 jit_solution(7123235884613912595)
XLA Ops:
  9.4 30.2 %scatter_custom_fusion.2 = bf16[12288,256]{1,0:T(8,128)(2,1)} fusion(s32[6144]{0:T(1024)S(1)} %bitcast.467, bf16[]{:T(256)} %constant.38.clone.1, bf16[768,256]{1,0:T(8,128)(2,1)S(1)} %copy.84), kind=kCustom, calls=%fused_computation.121 | custom fusion | bytes 6684674 | tf_op jit(solution)/shard_map/scatter | solution.py:72
  39.6 5.9 all-to-all-start.4
  47.5 33.0 %scatter_custom_fusion.3 = bf16[12288,256]{1,0:T(8,128)(2,1)} fusion(s32[6144]{0:T(1024)S(1)} %bitcast.469, f32[768,256]{1,0:T(8,128)S(1)} %copy.91, f32[6144]{0:T(1024)S(1)} %reshape.499, bf16[]{:T(256)} %constant.38.clone.1), kind=kCustom, calls=%fused_computation.98 | custom fusion | flops 3145728 | bytes 7102466 | tf_op jit(solution)/shard_map/scatter | solution.py:72
  80.4 36.8 %all-to-all-done.4 = bf16[8,1536,256]{2,1,0:T(8,128)(2,1)} async-done(((bf16[8,1536,256]{2,1,0:T(8,128)(2,1)}), bf16[8,1536,256]{2,1,0:T(8,128)(2,1)}, u32[]{:S(2)}, u32[]{:S(2)}) %all-to-all-start.4) | async-done | bytes 6291488 | tf_op jit(solution)/shard_map/all_to_all | solution.py:73
  117.2 5.1 all-to-all-start.6
  122.3 8.3 fusion.44
  130.6 9.2 fusion.16
  139.8 4.8 convert_bitcast_fusion
  148.1 45.7 %all-to-all-done.6 = bf16[8,1536,256]{2,1,0:T(8,128)(2,1)} async-done(((bf16[8,1536,256]{2,1,0:T(8,128)(2,1)}), bf16[8,1536,256]{2,1,0:T(8,128)(2,1)}, u32[]{:S(2)}, u32[]{:S(2)}) %all-to-all-start.6) | async-done | bytes 6291488 | tf_op jit(solution)/shard_map/all_to_all | solution.py:73
  193.8 5.3 all-to-all-start.5
  202.6 30.2 %scatter_custom_fusion = bf16[12288,256]{1,0:T(8,128)(2,1)} fusion(s32[6144]{0:T(1024)S(1)} %bitcast.472, bf16[]{:T(256)} %constant.38.clone.1, bf16[768,256]{1,0:T(8,128)(2,1)S(1)} %copy.70), kind=kCustom, calls=%fused_computation.125 | custom fusion | bytes 6684674 | tf_op jit(solution)/shard_map/scatter | solution.py:72
  232.8 37.9 %all-to-all-done.5 = bf16[8,1536,256]{2,1,0:T(8,128)(2,1)} async-done(((bf16[8,1536,256]{2,1,0:T(8,128)(2,1)}), bf16[8,1536,256]{2,1,0:T(8,128)(2,1)}, u32[]{:S(2)}, u32[]{:S(2)}) %all-to-all-start.5) | async-done | bytes 6291488 | tf_op jit(solution)/shard_map/all_to_all | solution.py:77
  270.7 4.9 all-to-all-start
  276.9 22.9 %gather_fusion.2 = bf16[6144,256]{1,0:T(8,128)(2,1)S(1)} fusion(bf16[12288,256]{1,0:T(8,128)(2,1)} %bitcast.66, s32[6144]{0:T(1024)S(1)} %broadcast_clamp_fusion.1), kind=kCustom, calls=%fused_computation.2 | custom fusion | bytes 6316032 | tf_op jit(solution)/shard_map/gather | solution.py:78
  299.9 6.0 multiply_reduce_fusion
  313.0 30.1 %scatter_custom_fusion.4 = bf16[12288,256]{1,0:T(8,128)(2,1)} fusion(s32[6144]{0:T(1024)S(1)} %bitcast.470, bf16[]{:T(256)} %constant.38.clone.1, bf16[768,256]{1,0:T(8,128)(2,1)S(1)} %copy.93), kind=kCustom, calls=%fused_computation.107 | custom fusion | bytes 6684674 | tf_op jit(solution)/shard_map/scatter | solution.py:72
  343.1 4.0 all-to-all-done
  347.1 5.2 all-to-all-start.7
  352.3 8.3 fusion.50
  360.5 10.0 %convert_bitcast_fusion.2 = bf16[8,48,32,256]{3,2,0,1:T(8,128)(2,1)} fusion(f32[48,8,32,128]{3,2,1,0:T(8,128)} %fusion.50, bf16[1,2,48,128,256]{4,3,2,1,0:T(8,128)(2,1)} %param.19, bf16[8,48,32,256]{3,2,1,0:T(8,128)(2,1)} %bitcast.7, bf16[1,2,48,256,128]{4,3,2,1,0:T(8,128)(2,1)} %param.17), kind=kOutput, calls=%fused_computation.73 | convolution fusion | flops 1623195648 | bytes 25165824 | tf_op jit(solution)/shard_map/secf,efd->secd/dot_general | solution.py:89
  370.6 6.5 copy.73
  377.1 46.7 %all-to-all-done.7 = bf16[8,1536,256]{2,1,0:T(8,128)(2,1)} async-done(((bf16[8,1536,256]{2,1,0:T(8,128)(2,1)}), bf16[8,1536,256]{2,1,0:T(8,128)(2,1)}, u32[]{:S(2)}, u32[]{:S(2)}) %all-to-all-start.7) | async-done | bytes 6291488 | tf_op jit(solution)/shard_map/all_to_all | solution.py:73
  423.8 4.9 all-to-all-start.1
  428.7 8.3 fusion.34
  437.0 7.3 fusion.36
  444.3 11.2 %fusion.14 = (bf16[8,48,32,128]{3,2,0,1:T(8,128)(2,1)}, bf16[8,48,32,128]{3,2,0,1:T(8,128)(2,1)}) fusion(f32[48,8,32,128]{3,2,1,0:T(8,128)} %fusion.34, f32[48,8,32,128]{3,2,1,0:T(8,128)} %fusion.36, bf16[1,2,48,128,256]{4,3,2,1,0:T(8,128)(2,1)} %param.19, bf16[8,48,32,256]{3,2,1,0:T(8,128)(2,1)} %bitcast.74), kind=kOutput, calls=%fused_computation.41 | convolution fusion | flops 825753600 | bytes 28311552 | tf_op jit(solution)/shard_map/secd,efd->secf/dot_general | solution.py:48
  455.5 8.5 fusion.61
  464.0 10.0 %fusion = bf16[8,48,32,256]{3,2,0,1:T(8,128)(2,1)} fusion(f32[48,8,32,256]{3,2,1,0:T(8,128)} %fusion.61, bf16[8,48,32,128]{3,2,0,1:T(8,128)(2,1)} %get-tuple-element.26, bf16[1,2,48,256,128]{4,3,2,1,0:T(8,128)(2,1)S(1)} %bitcast.445), kind=kOutput, calls=%fused_computation.16 | convolution fusion | flops 811597824 | bytes 25165824 | tf_op jit(solution)/shard_map/secf,edf->secd/dot_general | solution.py:54
  474.0 6.4 copy.96
  480.5 19.7 %all-to-all-done.1 = bf16[8,1536,256]{2,1,0:T(8,128)(2,1)} async-done(((bf16[8,1536,256]{2,1,0:T(8,128)(2,1)}), bf16[8,1536,256]{2,1,0:T(8,128)(2,1)}, u32[]{:S(2)}, u32[]{:S(2)}) %all-to-all-start.1) | async-done | bytes 6291488 | tf_op jit(solution)/shard_map/all_to_all | solution.py:77
  500.1 5.1 all-to-all-start.8
  508.2 22.9 %gather_fusion = bf16[6144,256]{1,0:T(8,128)(2,1)S(1)} fusion(bf16[12288,256]{1,0:T(8,128)(2,1)} %bitcast.21, s32[6144]{0:T(1024)S(1)} %broadcast_clamp_fusion.3), kind=kCustom, calls=%fused_computation | custom fusion | bytes 6316032 | tf_op jit(solution)/shard_map/gather | solution.py:78
  531.1 6.0 multiply_reduce_fusion.2
  542.6 30.2 %scatter_custom_fusion.1 = bf16[12288,256]{1,0:T(8,128)(2,1)} fusion(s32[6144]{0:T(1024)S(1)} %bitcast.471, bf16[]{:T(256)} %constant.38.clone.1, bf16[768,256]{1,0:T(8,128)(2,1)S(1)} %copy.76), kind=kCustom, calls=%fused_computation.123 | custom fusion | bytes 6684674 | tf_op jit(solution)/shard_map/scatter | solution.py:72
  572.8 3.9 all-to-all-done.8
  576.7 5.3 all-to-all-start.2
  583.4 22.9 %gather_fusion.3 = bf16[6144,256]{1,0:T(8,128)(2,1)S(1)} fusion(bf16[12288,256]{1,0:T(8,128)(2,1)} %bitcast.89, s32[6144]{0:T(1024)S(1)} %broadcast_clamp_fusion), kind=kCustom, calls=%fused_computation.3 | custom fusion | bytes 6316032 | tf_op jit(solution)/shard_map/gather | solution.py:78
  611.8 4.1 fusion.210
  617.3 32.8 %scatter_custom_fusion.5 = bf16[12288,256]{1,0:T(8,128)(2,1)} fusion(s32[6144]{0:T(1024)} %bitcast.468, f32[768,256]{1,0:T(8,128)S(1)} %copy.101, f32[6144]{0:T(1024)} %reshape.500, bf16[]{:T(256)} %constant.38.clone.1), kind=kCustom, calls=%fused_computation.99 | custom fusion | flops 3145728 | bytes 7102976 | tf_op jit(solution)/shard_map/scatter | solution.py:72
  650.1 3.5 all-to-all-done.2
  653.5 4.9 all-to-all-start.9
  658.5 8.2 fusion.46
  666.7 10.0 %convert_bitcast_fusion.1 = bf16[8,48,32,256]{3,2,0,1:T(8,128)(2,1)} fusion(f32[48,8,32,128]{3,2,1,0:T(8,128)} %fusion.46, bf16[1,2,48,128,256]{4,3,2,1,0:T(8,128)(2,1)} %param.19, bf16[8,48,32,256]{3,2,1,0:T(8,128)(2,1)} %bitcast.30, bf16[1,2,48,256,128]{4,3,2,1,0:T(8,128)(2,1)} %param.17), kind=kOutput, calls=%fused_computation.72 | convolution fusion | flops 1623195648 | bytes 25165824 | tf_op jit(solution)/shard_map/secf,efd->secd/dot_general | solution.py:89
  676.6 6.5 copy.79
  683.1 46.8 %all-to-all-done.9 = bf16[8,1536,256]{2,1,0:T(8,128)(2,1)} async-done(((bf16[8,1536,256]{2,1,0:T(8,128)(2,1)}), bf16[8,1536,256]{2,1,0:T(8,128)(2,1)}, u32[]{:S(2)}, u32[]{:S(2)}) %all-to-all-start.9) | async-done | bytes 6291488 | tf_op jit(solution)/shard_map/all_to_all | solution.py:73
  730.0 4.9 all-to-all-start.3
  736.2 11.2 %fusion.122 = f32[1,48,128,256]{3,2,1,0:T(8,128)} fusion(bf16[8,48,32,256]{3,2,1,0:T(8,128)(2,1)} %bitcast.74, f32[48,8,32,128]{3,2,1,0:T(8,128)} %fusion.36, f32[48,8,32,128]{3,2,1,0:T(8,128)} %fusion.34), kind=kOutput, calls=%fused_computation.161 | convolution fusion | flops 814743552 | bytes 25165824 | tf_op jit(solution)/shard_map/secf,secd->efd/dot_general | solution.py:51
  747.4 10.6 %fusion.4 = (bf16[8,48,32,128]{3,2,0,1:T(8,128)(2,1)}, bf16[8,48,32,128]{3,2,0,1:T(8,128)(2,1)S(1)}) fusion(f32[48,8,32,128]{3,2,1,0:T(8,128)} %fusion.44, f32[48,8,32,128]{3,2,1,0:T(8,128)} %get-tuple-element.56, bf16[1,2,48,128,256]{4,3,2,1,0:T(8,128)(2,1)} %param.19, bf16[8,48,32,256]{3,2,1,0:T(8,128)(2,1)} %bitcast.94), kind=kOutput, calls=%fused_computation.24 | convolution fusion | flops 825753600 | bytes 28311552 | tf_op jit(solution)/shard_map/secd,efd->secf/dot_general | solution.py:48
  757.9 9.6 %fusion.78 = f32[48,8,32,256]{3,2,1,0:T(8,128)} fusion(bf16[8,48,32,128]{3,2,0,1:T(8,128)(2,1)S(1)} %get-tuple-element.25, bf16[1,2,48,256,128]{4,3,2,1,0:T(8,128)(2,1)} %param.17), kind=kOutput, calls=%fused_computation.117 | convolution fusion | flops 805306368 | bytes 18874368 | tf_op jit(solution)/shard_map/secf,edf->secd/dot_general | solution.py:54
  767.6 10.1 %fusion.1 = bf16[8,48,32,256]{3,2,0,1:T(8,128)(2,1)} fusion(f32[48,8,32,256]{3,2,1,0:T(8,128)} %fusion.78, bf16[8,48,32,128]{3,2,0,1:T(8,128)(2,1)} %get-tuple-element.24, bf16[1,2,48,256,128]{4,3,2,1,0:T(8,128)(2,1)S(1)} %bitcast.447), kind=kOutput, calls=%fused_computation.17 | convolution fusion | flops 811597824 | bytes 25165824 | tf_op jit(solution)/shard_map/secf,edf->secd/dot_general | solution.py:54
  777.7 6.5 copy.103
  784.2 22.2 %all-to-all-done.3 = bf16[8,1536,256]{2,1,0:T(8,128)(2,1)} async-done(((bf16[8,1536,256]{2,1,0:T(8,128)(2,1)}), bf16[8,1536,256]{2,1,0:T(8,128)(2,1)}, u32[]{:S(2)}, u32[]{:S(2)}) %all-to-all-start.3) | async-done | bytes 6291488 | tf_op jit(solution)/shard_map/all_to_all | solution.py:77
  806.3 5.2 all-to-all-start.10
  811.6 7.3 fusion.119
  818.9 22.9 %gather_fusion.1 = bf16[6144,256]{1,0:T(8,128)(2,1)S(1)} fusion(bf16[12288,256]{1,0:T(8,128)(2,1)} %bitcast.44, s32[6144]{0:T(1024)S(1)} %broadcast_clamp_fusion.2), kind=kCustom, calls=%fused_computation.1 | custom fusion | bytes 6316032 | tf_op jit(solution)/shard_map/gather | solution.py:78
  841.9 6.0 multiply_reduce_fusion.1
  852.9 8.3 fusion.113
  863.6 6.6 fusion.127
  870.2 8.4 fusion.110
  878.6 7.4 fusion.116
  886.0 12.3 %maximum_bitcast_fusion = (f32[1,2,48,256,128]{4,3,2,1,0:T(8,128)}, f32[1,2,48,256,128]{4,3,2,1,0:T(8,128)}) fusion(f32[1,48,256,128]{3,2,1,0:T(8,128)S(1)} %bitcast.464, f32[1,48,256,128]{3,2,1,0:T(8,128)} %fusion.110, f32[1,48,256,128]{3,2,1,0:T(8,128)S(1)} %bitcast.462, f32[1,48,256,128]{3,2,1,0:T(8,128)} %fusion.116), kind=kLoop, calls=%fused_computation.11 | loop fusion | flops 6291456 | bytes 50331648 | tf_op jit(solution)/shard_map/broadcast_in_dim | solution.py:116
  898.4 23.2 %gather_fusion.4 = bf16[6144,256]{1,0:T(8,128)(2,1)S(1)} fusion(bf16[12288,256]{1,0:T(8,128)(2,1)} %bitcast.98, s32[6144]{0:T(1024)S(1)} %copy-done.1), kind=kCustom, calls=%fused_computation.4 | custom fusion | bytes 6316032 | tf_op jit(solution)/shard_map/gather | solution.py:78
  927.1 4.4 fusion.187
  933.7 11.0 %maximum_bitcast_fusion.2 = f32[1,2,48,128,256]{4,3,2,1,0:T(8,128)} fusion(f32[1,48,128,256]{3,2,1,0:T(8,128)} %fusion.122, f32[1,48,128,256]{3,2,1,0:T(8,128)} %fusion.127), kind=kLoop, calls=%fused_computation.13 | loop fusion | flops 3145728 | bytes 25165824 | tf_op jit(solution)/shard_map/broadcast_in_dim | solution.py:116
  (207 shorter events, 59.3 us)
Async XLA Ops:
  1.8 5.7 copy-start.6
  4.8 2.7 copy-start.19
  4.8 4.2 copy-start.26
  7.5 0.8 copy-start.8
  9.4 30.2 %copy-start.35 = (s32[6144,1]{0,1:T(1,128)}, s32[6144,1]{0,1:T(1,128)S(1)}, u32[]{:S(2)}) copy-start(s32[6144,1]{0,1:T(1,128)S(1)} %compare_select_fusion.1) | copy-start | bytes 73732
  39.6 6.3 copy-start.24
  39.6 6.8 copy-start.36
  39.6 77.6 %all-to-all-start.4 = ((bf16[8,1536,256]{2,1,0:T(8,128)(2,1)}), bf16[8,1536,256]{2,1,0:T(8,128)(2,1)}, u32[]{:S(2)}, u32[]{:S(2)}) async-start(bf16[8,1536,256]{2,1,0:T(8,128)(2,1)} %bitcast.454), calls=%async_computation.4 | async-start | bytes 12582912 | tf_op jit(solution)/shard_map/all_to_all | solution.py:73
  46.1 71.1 %copy-start.12 = (bf16[1,768,256]{1,2,0:T(8,128)(2,1)}, bf16[1,768,256]{1,2,0:T(8,128)(2,1)S(1)}, u32[]{:S(2)}) copy-start(bf16[1,768,256]{1,2,0:T(8,128)(2,1)S(1)} %copy.81) | copy-start | bytes 1179652
  117.2 13.5 %slice-start = ((s8[6291456]{0:T(1024)(128)(4,1)}), s8[2097152]{0:T(1024)(128)(4,1)S(1)}, s32[]{:S(2)}) async-start(s8[6291456]{0:T(1024)(128)(4,1)} %bitcast.442), calls=%async_computation.11 | async-start | bytes 4194304
  117.2 76.6 %all-to-all-start.6 = ((bf16[8,1536,256]{2,1,0:T(8,128)(2,1)}), bf16[8,1536,256]{2,1,0:T(8,128)(2,1)}, u32[]{:S(2)}, u32[]{:S(2)}) async-start(bf16[8,1536,256]{2,1,0:T(8,128)(2,1)} %bitcast.457), calls=%async_computation.6 | async-start | bytes 12582912 | tf_op jit(solution)/shard_map/all_to_all | solution.py:73
  122.3 8.3 slice-start.1
  139.8 4.8 copy-start.2
  193.8 5.4 copy-start.25
  193.8 5.7 copy-start.23
  193.8 76.9 %all-to-all-start.5 = ((bf16[8,1536,256]{2,1,0:T(8,128)(2,1)}), bf16[8,1536,256]{2,1,0:T(8,128)(2,1)}, u32[]{:S(2)}, u32[]{:S(2)}) async-start(bf16[8,1536,256]{2,1,0:T(8,128)(2,1)} %bitcast.452), calls=%async_computation.5 | async-start | bytes 12582912 | tf_op jit(solution)/shard_map/all_to_all | solution.py:77
  199.5 2.7 copy-start.27
  201.9 68.8 %copy-start.21 = (f32[768,256]{0,1:T(8,128)}, f32[768,256]{0,1:T(8,128)S(1)}, u32[]{:S(2)}) copy-start(f32[768,256]{0,1:T(8,128)S(1)} %get-tuple-element.50) | copy-start | bytes 2359300
  270.7 76.4 %all-to-all-start = ((bf16[8,1536,256]{2,1,0:T(8,128)(2,1)}), bf16[8,1536,256]{2,1,0:T(8,128)(2,1)}, u32[]{:S(2)}, u32[]{:S(2)}) async-start(bf16[8,1536,256]{2,1,0:T(8,128)(2,1)} %bitcast.450), calls=%async_computation | async-start | bytes 12582912 | tf_op jit(solution)/shard_map/all_to_all | solution.py:73
  276.9 23.0 %copy-start = (s32[6144]{0:T(1024)}, s32[6144]{0:T(1024)S(1)}, u32[]{:S(2)}) copy-start(s32[6144]{0:T(1024)S(1)} %broadcast_clamp_fusion.1) | copy-start | bytes 73732
  305.9 4.5 copy-start.41
  308.5 3.0 copy-start.10
  310.4 1.6 copy-start.20
  347.1 76.7 %all-to-all-start.7 = ((bf16[8,1536,256]{2,1,0:T(8,128)(2,1)}), bf16[8,1536,256]{2,1,0:T(8,128)(2,1)}, u32[]{:S(2)}, u32[]{:S(2)}) async-start(bf16[8,1536,256]{2,1,0:T(8,128)(2,1)} %bitcast.458), calls=%async_computation.7 | async-start | bytes 12582912 | tf_op jit(solution)/shard_map/all_to_all | solution.py:73
  423.8 13.2 %slice-start.2 = ((s8[6291456]{0:T(1024)(128)(4,1)}), s8[2097152]{0:T(1024)(128)(4,1)S(1)}, s32[]{:S(2)}) async-start(s8[6291456]{0:T(1024)(128)(4,1)} %bitcast.444), calls=%async_computation.13 | async-start | bytes 4194304
  423.8 76.4 %all-to-all-start.1 = ((bf16[8,1536,256]{2,1,0:T(8,128)(2,1)}), bf16[8,1536,256]{2,1,0:T(8,128)(2,1)}, u32[]{:S(2)}, u32[]{:S(2)}) async-start(bf16[8,1536,256]{2,1,0:T(8,128)(2,1)} %bitcast.455), calls=%async_computation.1 | async-start | bytes 12582912 | tf_op jit(solution)/shard_map/all_to_all | solution.py:77
  428.6 8.3 slice-start.3
  436.9 18.5 %slice-start.6 = ((s8[6291456]{0:T(1024)(128)(4,1)}), s8[4194304]{0:T(1024)(128)(4,1)S(1)}, s32[]{:S(2)}) async-start(s8[6291456]{0:T(1024)(128)(4,1)} %bitcast.459), calls=%async_computation.17 | async-start | bytes 8388608
  444.3 11.2 %slice-start.7 = ((s8[6291456]{0:T(1024)(128)(4,1)}), s8[2097152]{0:T(1024)(128)(4,1)S(1)}, s32[]{:S(2)}) async-start(s8[6291456]{0:T(1024)(128)(4,1)} %bitcast.459), calls=%async_computation.18 | async-start | bytes 4194304
  500.1 6.1 copy-start.37
  500.1 76.6 %all-to-all-start.8 = ((bf16[8,1536,256]{2,1,0:T(8,128)(2,1)}), bf16[8,1536,256]{2,1,0:T(8,128)(2,1)}, u32[]{:S(2)}, u32[]{:S(2)}) async-start(bf16[8,1536,256]{2,1,0:T(8,128)(2,1)} %bitcast.448), calls=%async_computation.8 | async-start | bytes 12582912 | tf_op jit(solution)/shard_map/all_to_all | solution.py:77
  542.4 34.3 %copy-start.22 = (f32[768,256]{0,1:T(8,128)}, f32[768,256]{0,1:T(8,128)S(1)}, u32[]{:S(2)}) copy-start(f32[768,256]{0,1:T(8,128)S(1)} %get-tuple-element.52) | copy-start | bytes 2359300
  576.7 5.7 copy-start.28
  576.7 76.8 %all-to-all-start.2 = ((bf16[8,1536,256]{2,1,0:T(8,128)(2,1)}), bf16[8,1536,256]{2,1,0:T(8,128)(2,1)}, u32[]{:S(2)}, u32[]{:S(2)}) async-start(bf16[8,1536,256]{2,1,0:T(8,128)(2,1)} %bitcast.449), calls=%async_computation.2 | async-start | bytes 12582912 | tf_op jit(solution)/shard_map/all_to_all | solution.py:73
  606.3 5.5 copy-start.11
  611.8 4.2 copy-start.40
  611.8 4.2 copy-start.13
  611.8 4.2 copy-start.15
  617.0 36.5 %copy-start.4 = (f32[768,256]{0,1:T(8,128)}, f32[768,256]{0,1:T(8,128)S(1)}, u32[]{:S(2)}) copy-start(f32[768,256]{0,1:T(8,128)S(1)} %fusion.247) | copy-start | bytes 2359300
  653.5 76.4 %all-to-all-start.9 = ((bf16[8,1536,256]{2,1,0:T(8,128)(2,1)}), bf16[8,1536,256]{2,1,0:T(8,128)(2,1)}, u32[]{:S(2)}, u32[]{:S(2)}) async-start(bf16[8,1536,256]{2,1,0:T(8,128)(2,1)} %bitcast.456), calls=%async_computation.9 | async-start | bytes 12582912 | tf_op jit(solution)/shard_map/all_to_all | solution.py:73
  730.0 4.9 copy-start.29
  730.0 5.3 copy-start.30
  730.0 76.4 %all-to-all-start.3 = ((bf16[8,1536,256]{2,1,0:T(8,128)(2,1)}), bf16[8,1536,256]{2,1,0:T(8,128)(2,1)}, u32[]{:S(2)}, u32[]{:S(2)}) async-start(bf16[8,1536,256]{2,1,0:T(8,128)(2,1)} %bitcast.453), calls=%async_computation.3 | async-start | bytes 12582912 | tf_op jit(solution)/shard_map/all_to_all | solution.py:77
  736.2 31.4 %slice-start.4 = ((s8[6291456]{0:T(1024)(128)(4,1)}), s8[2097152]{0:T(1024)(128)(4,1)S(1)}, s32[]{:S(2)}) async-start(s8[6291456]{0:T(1024)(128)(4,1)} %bitcast.446), calls=%async_computation.15 | async-start | bytes 4194304
  747.4 20.2 %slice-start.5 = ((s8[6291456]{0:T(1024)(128)(4,1)}), s8[4194304]{0:T(1024)(128)(4,1)S(1)}, s32[]{:S(2)}) async-start(s8[6291456]{0:T(1024)(128)(4,1)} %bitcast.446), calls=%async_computation.16 | async-start | bytes 8388608
  757.9 9.6 %copy-start.18 = (bf16[8,48,32,128]{3,2,0,1:T(8,128)(2,1)}, bf16[8,48,32,128]{3,2,0,1:T(8,128)(2,1)S(1)}, u32[]{:S(2)}) copy-start(bf16[8,48,32,128]{3,2,0,1:T(8,128)(2,1)S(1)} %get-tuple-element.25) | copy-start | bytes 9437188
  806.3 5.2 copy-start.16
  806.3 92.0 %all-to-all-start.10 = ((bf16[8,1536,256]{2,1,0:T(8,128)(2,1)}), bf16[8,1536,256]{2,1,0:T(8,128)(2,1)}, u32[]{:S(2)}, u32[]{:S(2)}) async-start(bf16[8,1536,256]{2,1,0:T(8,128)(2,1)} %bitcast.451), calls=%async_computation.10 | async-start | bytes 12582912 | tf_op jit(solution)/shard_map/all_to_all | solution.py:77
  850.5 13.1 %copy-start.3 = (bf16[8,48,32,128]{3,2,0,1:T(8,128)(2,1)S(1)}, bf16[8,48,32,128]{3,2,0,1:T(8,128)(2,1)}, u32[]{:S(2)}) copy-start(bf16[8,48,32,128]{3,2,0,1:T(8,128)(2,1)} %copy-done.2) | copy-start | bytes 9437188
  850.5 12.1 %collective-permute-start = (bf16[768,256]{0,1:T(8,128)(2,1)S(1)}, bf16[768,256]{0,1:T(8,128)(2,1)S(1)}, u32[]{:S(2)}, u32[]{:S(2)}) collective-permute-start(bf16[768,256]{0,1:T(8,128)(2,1)S(1)} %add_convert_fusion.2), channel_id=1, source_target_pairs={{0,8},{8,0},{1,9},{9,1},{2,10},{10,2},{3,11},{11,3},{4,12},{12,4},... | collective-permute-start | bytes 1179656 | tf_op jit(solution)/shard_map/ppermute | solution.py:114
  870.2 8.4 copy-start.17
  870.2 15.8 %slice-start.8 = ((s8[6291456]{0:T(1024)(128)(4,1)}), s8[4194304]{0:T(1024)(128)(4,1)S(1)}, s32[]{:S(2)}) async-start(s8[6291456]{0:T(1024)(128)(4,1)} %bitcast.461), calls=%async_computation.19 | async-start | bytes 8388608
  870.2 15.8 %slice-start.10 = ((s8[6291456]{0:T(1024)(128)(4,1)}), s8[4194304]{0:T(1024)(128)(4,1)S(1)}, s32[]{:S(2)}) async-start(s8[6291456]{0:T(1024)(128)(4,1)} %bitcast.463), calls=%async_computation.21 | async-start | bytes 8388608
  878.6 7.4 slice-start.9
  878.6 7.4 slice-start.11
  886.0 12.4 %copy-start.1 = (s32[6144]{0:T(1024)S(1)}, s32[6144]{0:T(1024)}, u32[]{:S(2)}) copy-start(s32[6144]{0:T(1024)} %copy-done) | copy-start | bytes 73732
  921.6 5.5 copy-start.34
  921.6 5.5 copy-start.39
  927.1 4.4 copy-start.5
  927.1 4.4 copy-start.7
  927.1 4.4 copy-start.9
  927.1 4.4 copy-start.32
  927.1 4.4 copy-start.38
  931.9 12.8 %collective-permute-start.1 = (bf16[768,256]{0,1:T(8,128)(2,1)S(1)}, bf16[768,256]{0,1:T(8,128)(2,1)S(1)}, u32[]{:S(2)}, u32[]{:S(2)}) collective-permute-start(bf16[768,256]{0,1:T(8,128)(2,1)S(1)} %fusion.186), channel_id=1, source_target_pairs={{0,8},{8,0},{1,9},{9,1},{2,10},{10,2},{3,11},{11,3},{4,12},{12,4},... | collective-permute-start | bytes 1179656 | tf_op jit(solution)/shard_map/ppermute | solution.py:115
  (3 other events, 1.9 us)
where the time goes:
time: 954 us; the launch traced here: 946 us
  local copies, waits for them, and re-layouts  286 us (30%)
  waiting for transfers between devices  268 us (28%)
  matrix products  204 us (21%)
  other arithmetic  124 us (13%)
  starting transfers between devices  60.9 us (6%)
    all_to_all x6, waiting for transfers between devices, dispatch(): lax.all_to_all(send_buf.reshape(groups, slots_dev, width), 'ep', 0, 0, ti...  183 us
    scatter x4, local copies, waits for them, and re-layouts, dispatch(): jnp.zeros((groups * slots_dev, width), rows.dtype).at[route.reshape(-1)]  121 us
    gather x5, local copies, waits for them, and re-layouts, combine(): return returned.reshape(groups * slots_dev, width)[route]  115 us
    all_to_all x5, waiting for transfers between devices, combine(): lax.all_to_all(rows.reshape(groups, slots_dev, width), 'ep', 0, 0, tiled=...  83.7 us
    scatter x2, other arithmetic, dispatch(): jnp.zeros((groups * slots_dev, width), rows.dtype).at[route.reshape(-1)]  65.7 us
    dot_general x4, matrix products, expert_front(): jnp.einsum('secd,edf->secf', received, w_up, preferred_element_type=jnp.f...  33 us
    all_to_all x6, starting transfers between devices, dispatch(): lax.all_to_all(send_buf.reshape(groups, slots_dev, width), 'ep', 0, 0, ti...  31.3 us
    all_to_all x5, starting transfers between devices, combine(): lax.all_to_all(rows.reshape(groups, slots_dev, width), 'ep', 0, 0, tiled=...  25.4 us
  transfers between devices with their start and end apart: 13, of which 11 were waited for; matrix products, arithmetic and copies ran while one was open for 57% of the time, Pallas kernels for 0%

commit v1 on v0

v1 whole, which is shorter than its diff:
```python
import jax
import jax.numpy as jnp
from jax import lax
from jax.experimental import pallas as pl
from jax.experimental.pallas import tpu as pltpu
from jax.sharding import PartitionSpec as P

MESH = pl.DeviceIdType.MESH
EPS = 1e-6
F32, BF16, I32 = jnp.float32, jnp.bfloat16, jnp.int32
T, D, FF, K = 768, 256, 1024, 8
G, E, C, F = 8, 48, 32, 128
S = E * C
NJ = S // 128
HALF = T // 2
ROWS = 256
B1, FW1, B2, FW2 = 0, 1, 2, 3
QF, QB = 4, 2


def dot(a, b):
    return jnp.dot(a, b, preferred_element_type=F32)


def dot_nt(a, b):
    return lax.dot_general(a, b, (((1,), (1,)), ((), ())), preferred_element_type=F32)


def dot_tn(a, b):
    return lax.dot_general(a, b, (((0,), (0,)), ((), ())), preferred_element_type=F32)


def rms_norm(v):
    return v * lax.rsqrt(jnp.mean(v * v, axis=-1, keepdims=True) + EPS)


def rms_back(v, g):
    inv = lax.rsqrt(jnp.mean(v * v, axis=-1, keepdims=True) + EPS)
    proj = jnp.mean(g * v, axis=-1, keepdims=True)
    return inv * g - v * (inv * inv * inv) * proj


def xor1(a, b):
    return a + b - 2 * a * b


def kernel(xf_h, xb_h, gin_h, win_h, wout_h, eg_h, eu_h, ed_h, rt_v, gt_v,
           y_o, dx_o, gg_o, gu_o, gd_o, zs_o,
           zall, slots, trow, tb, w1, w2, xv, hv, yv,
           osib, sib_in, mine, tree_in, fin_in, wgu, wd, dgg, dgu, dgd,
           ag_s, ag_r, ag_f, tb_s, tb_r, sb_s, sb_r, tr_s, tr_r, fi_s, fi_r,
           w_sem, g_sem, l_sem, o_s, o_r):
    pp, me = lax.axis_index("pp"), lax.axis_index("ep")
    my_y, my_x, my_c = lax.div(me, 4), lax.rem(lax.div(me, 2), 2), lax.rem(me, 2)
    ZB, ZF, GB = 0, 1, 2
    SB, SF, RO = 0, 1, 2
    XB, XF, XB2 = 0, 1, 2
    HB1, HF, HB2 = 0, 1, 2

    def peer(r):
        if isinstance(r, int):
            ry, rx, rc = r // 4, r // 2 % 2, r % 2
        else:
            ry, rx, rc = lax.div(r, 4), lax.rem(lax.div(r, 2), 2), lax.rem(r, 2)
        return xor1(my_y, ry) * 4 + xor1(my_x, rx) * 2 + xor1(my_c, rc)

    def dev(r):
        return {"pp": pp, "ep": peer(r)}

    def rcopy(src, dst, s_sem, r_sem, to):
        return pltpu.make_async_remote_copy(src_ref=src, dst_ref=dst, send_sem=s_sem, recv_sem=r_sem, device_id=to, device_id_type=MESH)

    barrier = pltpu.get_barrier_semaphore()
    for r in range(1, G):
        pl.semaphore_signal(barrier, inc=1, device_id=dev(r), device_id_type=MESH)
    stage_peer = {"pp": 1 - pp, "ep": me}
    pl.semaphore_signal(barrier, inc=1, device_id=stage_peer, device_id_type=MESH)

    local = [pltpu.make_async_copy(xb_h, xv.at[XB], l_sem.at[0]),
             pltpu.make_async_copy(xf_h, xv.at[XF], l_sem.at[1]),
             pltpu.make_async_copy(gin_h, zall.at[GB, me], l_sem.at[2]),
             pltpu.make_async_copy(win_h, w1, l_sem.at[3]),
             pltpu.make_async_copy(wout_h, w2, l_sem.at[4])]
    for c in local:
        c.start()
    local[0].wait()
    local[3].wait()
    local[4].wait()

    def ag_send(i, buf):
        block = zall.at[buf, me]
        for r in (6, 2, 4, 1):
            rcopy(block, block, ag_s.at[i, r], ag_r.at[i, r], dev(r)).start()

    def ag_wait(i, buf, r):
        src = zall.at[buf, peer(r)]
        rcopy(src, src, ag_s.at[i, r], ag_r.at[i, r], dev(1)).wait_recv()

        @pl.when(lax.rem(r, 2) == 0)
        def _():
            rcopy(src, src, ag_f.at[i, r], ag_r.at[i, r + 1], dev(1)).start()

    def ag_finish(i, buf):
        block = zall.at[buf, me]
        for r in (6, 2, 4, 1):
            rcopy(block, block, ag_s.at[i, r], ag_r.at[i, r], dev(r)).wait_send()
        for r in (2, 4, 6):
            src = zall.at[buf, peer(r)]
            rcopy(src, src, ag_f.at[i, r], ag_r.at[i, r + 1], dev(1)).wait_send()

    def dense_fwd(blk, x_ref, h_ref, z_ref):
        def body(i, _):
            rows = pl.ds(pl.multiple_of(i * ROWS, ROWS), ROWS)
            x = x_ref[rows, :].astype(F32)
            pre = dot(rms_norm(x).astype(BF16), w1[blk])
            h = (x + dot(jax.nn.silu(pre).astype(BF16), w2[blk])).astype(BF16)
            h_ref[rows, :] = h
            z_ref[rows, :] = rms_norm(h.astype(F32)).astype(BF16)
            return 0
        lax.fori_loop(0, T // ROWS, body, 0)

    def silu_grad(a):
        sig = jax.nn.sigmoid(a)
        return sig * (1.0 + a * (1.0 - sig))

    def dense_bwd(blk, x_ref, h_ref, g_ref, total, out_ref):
        def body(i, _):
            rows = pl.ds(pl.multiple_of(i * ROWS, ROWS), ROWS)
            x = x_ref[rows, :].astype(F32)
            pre = dot(rms_norm(x).astype(BF16), w1[blk])
            dh = g_ref[rows, :].astype(F32) + rms_back(h_ref[rows, :].astype(F32), total(rows))
            dm = dot_nt(dh.astype(BF16), w2[blk])
            dp = (dm * silu_grad(pre)).astype(BF16)
            out_ref[rows, :] = (dh + rms_back(x, dot_nt(dp, w1[blk]))).astype(BF16)
            return 0
        lax.fori_loop(0, T // ROWS, body, 0)

    def build_tables(first, last):
        def body(rt, _):
            acc_i = jnp.zeros((128, 128), F32)
            acc_g = jnp.zeros((128, 128), F32)
            for tc in range(T // 256):
                rows = rt_v[rt, :, tc * 256:(tc + 1) * 256]
                gates = gt_v[rt, :, tc * 256:(tc + 1) * 256]
                cols, gcols = rows.T, gates.T
                quad = lax.shift_right_logical(rows, 7)
                place = quad + 4 * lax.shift_right_logical(quad * 43, 9)
                lane = lax.bitwise_and(cols, 127)
                tok = lax.broadcasted_iota(I32, (256, 128), 0) + (tc * 256 + 1)
                low = lax.bitwise_and(tok, 255)
                high = (tok - low).astype(F32)
                low = low.astype(F32)
                lanes = lax.broadcasted_iota(I32, (256, 128), 1)
                spots = lax.broadcasted_iota(I32, (128, 256), 0)
                for k in range(K):
                    a = jnp.where(spots == place[k:k + 1, :], 1.0, 0.0).astype(BF16)
                    hit = lanes == lane[:, k:k + 1]
                    b = jnp.concatenate([jnp.where(hit, low, 0.0), jnp.where(hit, high, 0.0)], axis=1).astype(BF16)
                    both = dot(a, b)
                    acc_i += both[:, :128] + both[:, 128:]
                    acc_g += dot(a, jnp.where(hit, gcols[:, k:k + 1], 0.0).astype(BF16))
            trow[rt, :, 0] = acc_i.reshape(G, 16, 128)
            trow[rt, :, 1] = acc_g.reshape(G, 16, 128)
            tb[rt, me] = trow[rt, me]
            for r in range(1, G):
                rcopy(trow.at[rt, peer(r)], tb.at[rt, me], tb_s.at[rt, r], tb_r.at[rt, r], dev(r)).start()
            return 0
        lax.fori_loop(first, last, body, 0)

    def tables_wait(rt):
        for r in range(1, G):
            rcopy(trow.at[rt, peer(r)], tb.at[rt, peer(r)], tb_s.at[rt, r], tb_r.at[rt, r], dev(r)).wait()

    def dispatch(ag, buf, rt, dst, gated):
        def body(r, _):
            if ag is not None:
                @pl.when(r > 0)
                def _():
                    ag_wait(ag, buf, r)
            src = peer(r)
            z = zall[buf, src]
            cols = tb[rt, src, 0].T
            gcols = tb[rt, src, 1].T if gated else None
            base = pl.multiple_of(src * C, C)
            want = lax.broadcasted_iota(I32, (128, T), 1).astype(F32) + 1.0
            for j in range(0, NJ, 4):
                parts = []
                for q in range(j, j + 4):
                    val = gcols[:, q:q + 1] if gated else 1.0
                    parts.append(jnp.where(want == cols[:, q:q + 1], val, 0.0).astype(BF16))
                got = dot(jnp.concatenate(parts, axis=0), z).astype(BF16)
                slots[dst, 4 * j:4 * j + 16, pl.ds(base, C), :] = got.reshape(16, C, D)
            return 0
        lax.fori_loop(0, G, body, 0)
        if ag is not None:
            ag_finish(ag, buf)

    def w_copies(blk, i, slot, q):
        es = pl.ds(i * q, q)
        return [pltpu.make_async_copy(eg_h.at[blk, es], wgu.at[slot, pl.ds(0, q), :, pl.ds(0, F)], w_sem.at[slot, 0]),
                pltpu.make_async_copy(eu_h.at[blk, es], wgu.at[slot, pl.ds(0, q), :, pl.ds(F, F)], w_sem.at[slot, 1]),
                pltpu.make_async_copy(ed_h.at[blk, es], wd.at[slot, pl.ds(0, q)], w_sem.at[slot, 2])]

    def w_first(blk, q):
        for c in w_copies(blk, 0, 0, q):
            c.start()

    def experts_fwd(blk, src, dst):
        steps = E // QF

        def body(i, _):
            slot = lax.rem(i, 2)

            @pl.when(i + 1 < steps)
            def _():
                for c in w_copies(blk, i + 1, 1 - slot, QF):
                    c.start()
            for c in w_copies(blk, i, slot, QF):
                c.wait()
            for n in range(QF):
                e = i * QF + n
                gu = dot(slots[src, e], wgu[slot, n])
                mid = (jax.nn.silu(gu[:, :F]) * gu[:, F:]).astype(BF16)
                slots[dst, e] = dot(mid, wd[slot, n]).astype(BF16)
            return 0
        lax.fori_loop(0, steps, body, 0)

    def g_copies(blk, i, slot):
        es = pl.ds(i * QB, QB)
        return [pltpu.make_async_copy(dgg.at[slot], gg_o.at[blk, es], g_sem.at[slot, 0]),
                pltpu.make_async_copy(dgu.at[slot], gu_o.at[blk, es], g_sem.at[slot, 1]),
                pltpu.make_async_copy(dgd.at[slot], gd_o.at[blk, es], g_sem.at[slot, 2])]

    def experts_bwd(blk, zsrc, ro):
        steps = E // QB

        def body(i, _):
            slot = lax.rem(i, 2)

            @pl.when(i + 1 < steps)
            def _():
                for c in w_copies(blk, i + 1, 1 - slot, QB):
                    c.start()
            for c in w_copies(blk, i, slot, QB):
                c.wait()

            @pl.when(i >= 2)
            def _():
                for c in g_copies(blk, i - 2, slot):
                    c.wait()
            for n in range(QB):
                e = i * QB + n
                z, rr = slots[zsrc, e], slots[ro, e]
                gu = dot(z, wgu[slot, n])
                a, b = gu[:, :F], gu[:, F:]
                sig = jax.nn.sigmoid(a)
                act = a * sig
                mid = (act * b).astype(BF16)
                dm = dot_nt(rr, wd[slot, n])
                da = (dm * b * (sig * (1.0 + a * (1.0 - sig)))).astype(BF16)
                db = (dm * act).astype(BF16)
                dab = jnp.concatenate([da, db], axis=1)
                dgd[slot, n] = dot_tn(mid, rr)
                dw = dot_tn(z, dab)
                dgg[slot, n] = dw[:, :F]
                dgu[slot, n] = dw[:, F:]
                slots[ro, e] = dot_nt(dab, wgu[slot, n]).astype(BF16)
            for c in g_copies(blk, i, slot):
                c.start()
            return 0
        lax.fori_loop(0, steps, body, 0)
        for i in (steps - 2, steps - 1):
            for c in g_copies(blk, i, i % 2):
                c.wait()

    def combine(rs, ch, rt, src, gated):
        def rows_of(s):
            vals = slots[src, :, pl.ds(pl.multiple_of(s * C, C), C), :].reshape(S, D)
            want = lax.broadcasted_iota(I32, (T, 128), 0).astype(F32) + 1.0
            parts = []
            for j in range(NJ):
                val = tb[rt, s, 1, j:j + 1, :] if gated else 1.0
                parts.append(jnp.where(want == tb[rt, s, 0, j:j + 1, :], val, 0.0).astype(BF16))
            return dot(jnp.concatenate(parts, axis=1), vals)

        def sib_copy(q, n):
            return rcopy(osib.at[ch, n], sib_in.at[ch, q], sb_s.at[rs, q], sb_r.at[rs, q], dev(1))

        def body(n, _):
            q = 3 - n

            @pl.when(n >= 2)
            def _():
                sib_copy(q + 2, lax.rem(n, 2)).wait_send()
            osib[ch, lax.rem(n, 2)] = rows_of(peer(2 * q + 1))
            sib_copy(q, lax.rem(n, 2)).start()
            own = rows_of(peer(2 * q))
            sib_copy(q, lax.rem(n, 2)).wait_recv()
            mine[ch, q] = own + sib_in[ch, q]

            @pl.when(n == 0)
            def _():
                for c in tree(rs, ch):
                    c.start()

            @pl.when(n == 1)
            def _():
                fin(rs, ch, 1, 1).start()

            @pl.when(n == 2)
            def _():
                fin(rs, ch, 0, 0).start()
            return 0
        lax.fori_loop(0, 4, body, 0)
        for n in (2, 3):
            sib_copy(3 - n, n % 2).wait_send()
        first, second = tree(rs, ch)
        first.wait()
        mine[ch, 2, 0:HALF] += tree_in[ch, 0]
        fin(rs, ch, 1, 0).start()
        second.wait()
        mine[ch, 1, HALF:T] += tree_in[ch, 1]
        fin(rs, ch, 0, 1).start()

    def tree(rs, ch):
        return [rcopy(mine.at[ch, 3, pl.ds(0, HALF)], tree_in.at[ch, 0], tr_s.at[rs, 0], tr_r.at[rs, 0], dev(2)),
                rcopy(mine.at[ch, 3, pl.ds(HALF, HALF)], tree_in.at[ch, 1], tr_s.at[rs, 1], tr_r.at[rs, 1], dev(4))]

    def fin(rs, ch, axis, half):
        rows = pl.ds(half * HALF, HALF)
        return rcopy(mine.at[ch, 1 + axis, rows], fin_in.at[ch, axis, rows], fi_s.at[rs, axis, half], fi_r.at[rs, axis, half], dev(2 + 2 * axis))

    def rs_wait(rs, ch):
        for axis in range(2):
            for half in range(2):
                fin(rs, ch, axis, half).wait()

    def total_of(ch):
        return lambda rows: mine[ch, 0, rows, :] + fin_in[ch, 0, rows, :] + fin_in[ch, 1, rows, :]

    def block_out(ch, h_ref, out_ref):
        total = total_of(ch)

        def body(i, _):
            rows = pl.ds(pl.multiple_of(i * ROWS, ROWS), ROWS)
            out_ref[rows, :] = (h_ref[rows, :].astype(F32) + total(rows)).astype(BF16)
            return 0
        lax.fori_loop(0, T // ROWS, body, 0)

    w_first(0, QF)
    dense_fwd(0, xv.at[XB], hv.at[HB1], zall.at[ZB, me])
    pl.semaphore_wait(barrier, G)
    ag_send(0, ZB)
    build_tables(0, 1)
    local[1].wait()
    dense_fwd(0, xv.at[XF], hv.at[HF], zall.at[ZF, me])
    ag_send(1, ZF)
    local[2].wait()
    ag_send(2, GB)
    build_tables(1, 4)

    tables_wait(B1)
    dispatch(0, ZB, B1, SB, False)
    save = pltpu.make_async_copy(slots.at[SB], zs_o, l_sem.at[0])
    save.start()
    experts_fwd(0, SB, RO)
    w_first(0, QF)
    combine(0, 0, B1, RO, True)

    tables_wait(FW1)
    dispatch(1, ZF, FW1, SF, False)
    experts_fwd(0, SF, SF)
    w_first(1, QB)
    combine(1, 1, FW1, SF, True)

    rs_wait(0, 0)
    block_out(0, hv.at[HB1], xv.at[XB2])
    dense_fwd(1, xv.at[XB2], hv.at[HB2], zall.at[ZB, me])
    ag_send(3, ZB)
    tables_wait(B2)
    dispatch(2, GB, B2, RO, True)
    rs_wait(1, 1)
    block_out(1, hv.at[HF], xv.at[XF])
    dense_fwd(1, xv.at[XF], hv.at[HF], zall.at[ZF, me])
    ag_send(4, ZF)

    save.wait()
    dispatch(3, ZB, B2, SB, False)
    experts_bwd(1, SB, RO)
    w_first(1, QF)
    load = pltpu.make_async_copy(zs_o, slots.at[SB], l_sem.at[1])
    load.start()
    combine(2, 0, B2, RO, False)

    tables_wait(FW2)
    dispatch(4, ZF, FW2, SF, False)
    experts_fwd(1, SF, SF)
    w_first(0, QB)
    combine(3, 1, FW2, SF, True)

    rs_wait(2, 0)
    dense_bwd(1, xv.at[XB2], hv.at[HB2], zall.at[GB, me], total_of(0), zall.at[ZB, me])
    ag_send(5, ZB)
    rs_wait(3, 1)
    block_out(1, hv.at[HF], yv.at[0])
    send_y = rcopy(yv.at[0], y_o, o_s.at[0], o_r.at[0], stage_peer)
    send_y.start()

    dispatch(5, ZB, B1, RO, True)
    load.wait()
    experts_bwd(0, SB, RO)
    combine(4, 0, B1, RO, False)
    rs_wait(4, 0)
    dense_bwd(0, xv.at[XB], hv.at[HB1], zall.at[ZB, me], total_of(0), yv.at[1])
    send_x = rcopy(yv.at[1], dx_o, o_s.at[1], o_r.at[1], stage_peer)
    send_x.start()
    send_y.wait()
    send_x.wait()


def solution(mesh):
    def local_step(x_fwd, x_bwd, grad_in, dense_in, dense_out, exp_gate, exp_up, exp_down, route_fwd, gate_fwd, route_bwd, gate_bwd):
        route = jnp.stack([route_bwd[0, 0], route_fwd[0, 0], route_bwd[0, 1], route_fwd[0, 1]]).transpose(0, 2, 1)
        gate = jnp.stack([gate_bwd[0, 0], gate_fwd[0, 0], gate_bwd[0, 1], gate_fwd[0, 1]]).astype(F32).transpose(0, 2, 1)
        vmem, hbm = pl.BlockSpec(memory_space=pltpu.VMEM), pl.BlockSpec(memory_space=pl.ANY)
        dma = pltpu.SemaphoreType.DMA
        tok = jax.ShapeDtypeStruct((T, D), BF16)
        up = jax.ShapeDtypeStruct((2, E, D, F), F32)
        down = jax.ShapeDtypeStruct((2, E, F, D), F32)
        outs = pl.pallas_call(
            kernel,
            out_shape=(tok, tok, up, up, down, jax.ShapeDtypeStruct((E, G * C, D), BF16)),
            in_specs=[hbm] * 8 + [vmem] * 2,
            out_specs=(vmem, vmem, hbm, hbm, hbm, hbm),
            scratch_shapes=[
                pltpu.VMEM((3, G, T, D), BF16),
                pltpu.VMEM((3, E, G * C, D), BF16),
                pltpu.VMEM((4, G, 2, 16, 128), F32),
                pltpu.VMEM((4, G, 2, 16, 128), F32),
                pltpu.VMEM((2, D, FF), BF16),
                pltpu.VMEM((2, FF, D), BF16),
                pltpu.VMEM((3, T, D), BF16),
                pltpu.VMEM((3, T, D), BF16),
                pltpu.VMEM((2, T, D), BF16),
                pltpu.VMEM((2, 2, T, D), F32),
                pltpu.VMEM((2, 4, T, D), F32),
                pltpu.VMEM((2, 4, T, D), F32),
                pltpu.VMEM((2, 2, HALF, D), F32),
                pltpu.VMEM((2, 2, T, D), F32),
                pltpu.VMEM((2, QF, D, 2 * F), BF16),
                pltpu.VMEM((2, QF, F, D), BF16),
                pltpu.VMEM((2, QB, D, F), F32),
                pltpu.VMEM((2, QB, D, F), F32),
                pltpu.VMEM((2, QB, F, D), F32),
                dma((6, 8)), dma((6, 8)), dma((6, 8)),
                dma((4, 8)), dma((4, 8)),
                dma((5, 4)), dma((5, 4)), dma((5, 2)), dma((5, 2)), dma((5, 2, 2)), dma((5, 2, 2)),
                dma((2, 3)), dma((2, 3)), dma((5,)), dma((2,)), dma((2,)),
            ],
            compiler_params=pltpu.CompilerParams(collective_id=0, has_side_effects=True, vmem_limit_bytes=67043328),
        )(x_fwd[0], x_bwd[0], grad_in[0], dense_in[0], dense_out[0], exp_gate[0], exp_up[0], exp_down[0], route, gate)
        y_next, dx_prev, dgate, dup, ddown = outs[:5]
        return y_next[None], dx_prev[None], dgate[None], dup[None], ddown[None]

    tok_spec = P('pp', 'ep', None)
    dense_spec = P('pp', None, None, None)
    exp_spec = P('pp', None, 'ep', None, None)
    route_spec = P('pp', None, 'ep', None)
    return jax.shard_map(local_step, mesh=mesh, in_specs=(tok_spec, tok_spec, tok_spec, dense_spec, dense_spec, exp_spec, exp_spec, exp_spec, route_spec, route_spec, route_spec, route_spec), out_specs=(tok_spec, tok_spec, exp_spec, exp_spec, exp_spec), check_vma=False)
```

time: 954 us -> 395 us (0.41)
  Pallas kernels: 0 us -> 353 us
  waiting for transfers between devices: 268 us -> 0 us
  local copies, waits for them, and re-layouts: 286 us -> 37.9 us
  matrix products: 204 us -> 0 us
  other arithmetic: 124 us -> 1.3 us
  starting transfers between devices: 60.9 us -> 0 us
    pallas_call x0 -> x1, Pallas kernels: none -> 353 us  [local_step(): pl.pallas_call(kernel, out_shape=(tok, tok, up, up, down, jax.ShapeDtypeS...]
    all_to_all x11 -> x0, waiting for transfers between devices: 267 us -> none  [the longest x6 183 us: dispatch(): lax.all_to_all(send_buf.reshape(groups, slots_dev, width), 'ep', 0, 0, ti...]
    dot_general x29 -> x0, matrix products: 204 us -> none  [the longest x4 33 us: expert_front(): jnp.einsum('secd,edf->secf', received, w_up, preferred_element_type=jnp.f...]
    scatter x4 -> x0, local copies, waits for them, and re-layouts: 121 us -> none  [dispatch(): jnp.zeros((groups * slots_dev, width), rows.dtype).at[route.reshape(-1)]]
    gather x5 -> x0, local copies, waits for them, and re-layouts: 115 us -> none  [combine(): return returned.reshape(groups * slots_dev, width)[route]]
    scatter x2 -> x0, other arithmetic: 65.7 us -> none  [dispatch(): jnp.zeros((groups * slots_dev, width), rows.dtype).at[route.reshape(-1)]]
    all_to_all x11 -> x0, starting transfers between devices: 56.7 us -> none  [the longest x6 31.3 us: dispatch(): lax.all_to_all(send_buf.reshape(groups, slots_dev, width), 'ep', 0, 0, ti...]
    convert_element_type x15 -> x0, local copies, waits for them, and re-layouts: 31.9 us -> none  [the longest x3 16.4 us: block_finish(): jnp.einsum('secf,efd->secd', saved[6], weights[4], preferred_element_type...]
  transfers between devices with their start and end apart: 13 -> 0, of which waited for: 11 -> 0; matrix products, arithmetic and copies ran while one was open for 57% -> 0% of each run, Pallas kernels for 0% -> 0%
where the time goes in v1:
time: 395 us; the launch traced here: 393 us
  Pallas kernels  353 us (89%)
  local copies, waits for them, and re-layouts  37.9 us (10%)
    pallas_call x1, Pallas kernels, local_step(): pl.pallas_call(kernel, out_shape=(tok, tok, up, up, down, jax.ShapeDtypeS...  353 us
    unnamed x5, local copies, waits for them, and re-layouts  36.3 us

profile of v1, /device:TPU:0, one launch (start us, length us, event | category | flops | bytes accessed | tf_op | source)
XLA Modules:
  0.0 393.0 jit_solution(11983189921374258954)
XLA Ops:
  0.6 0.8 slice_bitcast_fusion.6
  1.4 0.7 convert_bitcast_fusion.gt_v
  2.0 0.8 slice_bitcast_fusion.2
  2.8 0.6 add_bitcast_fusion.rt_v
  3.5 353.2 %shard_map.155 = (bf16[768,256]{1,0:T(8,128)(2,1)}, bf16[768,256]{1,0:T(8,128)(2,1)}, f32[2,48,256,128]{3,2,1,0:T(8,128)}, f32[2,48,256,128]{3,2,1,0:T(8,128)}, ...) custom-call(bf16[768,256]{1,0:T(8,128)(2,1)} %bitcast.43, bf16[768,256]{1,0:T(8,128)(2,1)} %bitcast.44, ...), custom_call_target="tpu_custom_call" | custom-call | tf_op jit(solution)/shard_map/pallas_call | solution.py:430
  356.7 1.8 copy.22
  358.5 1.8 copy.23
  360.3 10.9 %copy.24 = f32[1,2,48,256,128]{4,3,2,1,0:T(8,128)} copy(f32[1,2,48,256,128]{4,3,2,1,0:T(8,128)} %bitcast.35) | data formatting | bytes 25165824
  371.2 10.9 %copy.25 = f32[1,2,48,256,128]{4,3,2,1,0:T(8,128)} copy(f32[1,2,48,256,128]{4,3,2,1,0:T(8,128)} %bitcast.34) | data formatting | bytes 25165824
  382.1 10.9 %copy.26 = f32[1,2,48,128,256]{4,3,2,1,0:T(8,128)} copy(f32[1,2,48,128,256]{4,3,2,1,0:T(8,128)} %bitcast.33) | data formatting | bytes 25165824

commit v2 on v1

v2 whole, which is shorter than its diff:
```python
import jax
import jax.numpy as jnp
from jax import lax
from jax.experimental import pallas as pl
from jax.experimental.pallas import tpu as pltpu
from jax.sharding import PartitionSpec as P

MESH = pl.DeviceIdType.MESH
EPS = 1e-6
F32, BF16, I32 = jnp.float32, jnp.bfloat16, jnp.int32
T, D, FF, K = 768, 256, 1024, 8
G, E, C, F = 8, 48, 32, 128
S = E * C
NJ = S // 128
HALF = T // 2
ROWS = 256
B1, FW1, B2, FW2 = range(4)
SIB, XN, YN, DIAG = 1, 2, 4, 6
LOW, UP = 0, 1
BB, FB = 0, 1
Q, AHEAD = 8, 2
STEPS = E // Q


def dot(a, b):
    return jnp.dot(a, b, preferred_element_type=F32)


def dot_nt(a, b):
    return lax.dot_general(a, b, (((1,), (1,)), ((), ())), preferred_element_type=F32)


def dot_tn(a, b):
    return lax.dot_general(a, b, (((0,), (0,)), ((), ())), preferred_element_type=F32)


def rms_norm(v):
    return v * lax.rsqrt(jnp.mean(v * v, axis=-1, keepdims=True) + EPS)


def rms_back(v, g):
    inv = lax.rsqrt(jnp.mean(v * v, axis=-1, keepdims=True) + EPS)
    proj = jnp.mean(g * v, axis=-1, keepdims=True)
    return inv * g - v * (inv * inv * inv) * proj


def xor1(a, b):
    return a + b - 2 * a * b


def kernel(xf_h, xb_h, gin_h, win_h, wout_h, eg_h, eu_h, ed_h, rt_v, gt_v,
           y_o, dx_o, z_o, r_o, dab_o, mid_o,
           zall, slots, trow, tb, w1, w2, xv, hv, yv,
           part, sib_in, tree_in, fin_in, wgu, wd, dab_v, mid_v,
           ag_s, ag_r, tb_s, tb_r, sb_s, sb_r, tr_s, tr_r, fi_s, fi_r,
           w_sem, g_sem, l_sem, o_s, o_r):
    pp, me = lax.axis_index("pp"), lax.axis_index("ep")
    my_y, my_x, my_c = lax.div(me, 4), lax.rem(lax.div(me, 2), 2), lax.rem(me, 2)
    ZB, ZF, GB = range(3)
    SB, SF, RO = range(3)
    XB, XF, XB2 = range(3)
    HB1, HF, HB2 = range(3)

    def peer(r):
        if isinstance(r, int):
            ry, rx, rc = r // 4, r // 2 % 2, r % 2
        else:
            ry, rx, rc = lax.div(r, 4), lax.rem(lax.div(r, 2), 2), lax.rem(r, 2)
        return xor1(my_y, ry) * 4 + xor1(my_x, rx) * 2 + xor1(my_c, rc)

    def dev(r):
        return {"pp": pp, "ep": peer(r)}

    def rcopy(src, dst, s_sem, r_sem, to):
        return pltpu.make_async_remote_copy(src_ref=src, dst_ref=dst, send_sem=s_sem, recv_sem=r_sem, device_id=to, device_id_type=MESH)

    barrier = pltpu.get_barrier_semaphore()
    for r in range(1, G):
        pl.semaphore_signal(barrier, inc=1, device_id=dev(r), device_id_type=MESH)
    stage_peer = {"pp": 1 - pp, "ep": me}
    pl.semaphore_signal(barrier, inc=1, device_id=stage_peer, device_id_type=MESH)

    pairs = [(xb_h, xv.at[XB]), (win_h, w1), (wout_h, w2), (xf_h, xv.at[XF]), (gin_h, zall.at[GB, me])]
    local = [pltpu.make_async_copy(src, dst, l_sem.at[n]) for n, (src, dst) in enumerate(pairs)]
    for c in local:
        c.start()
    load_xb, load_w1, load_w2, load_xf, load_g = local
    for c in (load_xb, load_w1, load_w2):
        c.wait()

    def half(buf, r, h):
        return zall.at[buf, me if r is None else peer(r), pl.ds(h * HALF, HALF)]

    def ag_copy(i, n, ref, r):
        return rcopy(ref, ref, ag_s.at[i, n], ag_r.at[i, n], dev(r))

    X_LOW, X_UP, Y_LOW, Y_UP, OWN, D_LOW, D_UP, PASS = range(8)

    def ag_own(i, buf):
        low, up = half(buf, None, LOW), half(buf, None, UP)
        return [ag_copy(i, X_LOW, low, XN), ag_copy(i, Y_UP, up, YN), ag_copy(i, X_UP, up, XN), ag_copy(i, Y_LOW, low, YN),
                ag_copy(i, OWN, zall.at[buf, me], SIB)]

    def ag_pass(i, buf):
        return ag_copy(i, D_LOW, half(buf, XN, LOW), YN), ag_copy(i, D_UP, half(buf, YN, UP), XN)

    def ag_sib(i, buf, n):
        return ag_copy(i, PASS + n, zall.at[buf, peer((XN, YN, DIAG)[n])], SIB)

    def ag_send(i, buf):
        for c in ag_own(i, buf):
            c.start()

    def ag_mid(i, buf):
        first, second = ag_pass(i, buf)
        ag_copy(i, X_LOW, half(buf, XN, LOW), XN).wait_recv()
        first.start()
        ag_copy(i, Y_UP, half(buf, YN, UP), YN).wait_recv()
        second.start()

    def ag_step(i, buf, r):
        waits = [[(OWN, zall.at[buf, peer(SIB)]), (X_UP, half(buf, XN, UP))],
                 [(PASS, zall.at[buf, peer(XN + SIB)]), (Y_LOW, half(buf, YN, LOW))],
                 [(PASS + 1, zall.at[buf, peer(YN + SIB)]), (D_LOW, half(buf, DIAG, LOW)), (D_UP, half(buf, DIAG, UP))],
                 [(PASS + 2, zall.at[buf, peer(DIAG + SIB)])]]
        for n, group in enumerate(waits):
            @pl.when(r == 2 * n + 1)
            def _(n=n, group=group):
                for sem, ref in group:
                    ag_copy(i, sem, ref, SIB).wait_recv()
                if len(group) > 1:
                    ag_sib(i, buf, n).start()

    def ag_finish(i, buf):
        for c in ag_own(i, buf) + list(ag_pass(i, buf)):
            c.wait_send()
        for n in range(3):
            ag_sib(i, buf, n).wait_send()

    def dense_fwd(blk, x_ref, h_ref, z_ref):
        def body(i, _):
            rows = pl.ds(pl.multiple_of(i * ROWS, ROWS), ROWS)
            x = x_ref[rows, :].astype(F32)
            pre = dot(rms_norm(x).astype(BF16), w1[blk])
            h = (x + dot(jax.nn.silu(pre).astype(BF16), w2[blk])).astype(BF16)
            h_ref[rows, :] = h
            z_ref[rows, :] = rms_norm(h.astype(F32)).astype(BF16)
            return 0
        lax.fori_loop(0, T // ROWS, body, 0)

    def silu_grad(a):
        sig = jax.nn.sigmoid(a)
        return sig * (1.0 + a * (1.0 - sig))

    def dense_bwd(blk, x_ref, h_ref, g_ref, total, out_ref):
        def body(i, _):
            rows = pl.ds(pl.multiple_of(i * ROWS, ROWS), ROWS)
            x = x_ref[rows, :].astype(F32)
            pre = dot(rms_norm(x).astype(BF16), w1[blk])
            dh = g_ref[rows, :].astype(F32) + rms_back(h_ref[rows, :].astype(F32), total(rows))
            dm = dot_nt(dh.astype(BF16), w2[blk])
            dp = (dm * silu_grad(pre)).astype(BF16)
            out_ref[rows, :] = (dh + rms_back(x, dot_nt(dp, w1[blk]))).astype(BF16)
            return 0
        lax.fori_loop(0, T // ROWS, body, 0)

    def build_tables(first, last):
        def body(rt, _):
            acc_i = jnp.zeros((128, 128), F32)
            acc_g = jnp.zeros((128, 128), F32)
            for tc in range(T // 256):
                rows = rt_v[rt, :, tc * 256:(tc + 1) * 256]
                gates = gt_v[rt, :, tc * 256:(tc + 1) * 256]
                cols, gcols = rows.T, gates.T
                quad = lax.shift_right_logical(rows, 7)
                place = quad + 4 * lax.shift_right_logical(quad * 43, 9)
                lane = lax.bitwise_and(cols, 127)
                tok = lax.broadcasted_iota(I32, (256, 128), 0) + (tc * 256 + 1)
                low = lax.bitwise_and(tok, 255)
                high = (tok - low).astype(F32)
                low = low.astype(F32)
                lanes = lax.broadcasted_iota(I32, (256, 128), 1)
                spots = lax.broadcasted_iota(I32, (128, 256), 0)
                for k in range(K):
                    a = jnp.where(spots == place[k:k + 1, :], 1.0, 0.0).astype(BF16)
                    hit = lanes == lane[:, k:k + 1]
                    b = jnp.concatenate([jnp.where(hit, low, 0.0), jnp.where(hit, high, 0.0)], axis=1).astype(BF16)
                    both = dot(a, b)
                    acc_i += both[:, :128] + both[:, 128:]
                    acc_g += dot(a, jnp.where(hit, gcols[:, k:k + 1], 0.0).astype(BF16))
            trow[rt, :, 0] = acc_i.reshape(G, 16, 128)
            trow[rt, :, 1] = acc_g.reshape(G, 16, 128)
            tb[rt, me] = trow[rt, me]
            return 0
        lax.fori_loop(first, last, body, 0)

    def tables_send(rt):
        for r in range(1, G):
            rcopy(trow.at[rt, peer(r)], tb.at[rt, me], tb_s.at[rt, r], tb_r.at[rt, r], dev(r)).start()

    def tables_wait(rt):
        for r in range(1, G):
            rcopy(trow.at[rt, peer(r)], tb.at[rt, peer(r)], tb_s.at[rt, r], tb_r.at[rt, r], dev(r)).wait()

    def dispatch(ag, buf, rt, dst, gated):
        def body(r, _):
            if ag is not None:
                ag_step(ag, buf, r)
            src = peer(r)
            z = zall[buf, src]
            cols = tb[rt, src, 0].T
            gcols = tb[rt, src, 1].T if gated else None
            base = pl.multiple_of(src * C, C)
            want = lax.broadcasted_iota(I32, (128, T), 1).astype(F32) + 1.0
            for j in range(0, NJ, 4):
                parts = []
                for q in range(j, j + 4):
                    val = gcols[:, q:q + 1] if gated else 1.0
                    parts.append(jnp.where(want == cols[:, q:q + 1], val, 0.0).astype(BF16))
                got = dot(jnp.concatenate(parts, axis=0), z).astype(BF16)
                slots[dst, 4 * j:4 * j + 16, pl.ds(base, C), :] = got.reshape(16, C, D)
            return 0
        lax.fori_loop(0, G, body, 0)
        if ag is not None:
            ag_finish(ag, buf)

    def w_copies(blk, i):
        slot = i % (AHEAD + 1) if isinstance(i, int) else lax.rem(i, AHEAD + 1)
        es = pl.ds(i * Q, Q)
        return [pltpu.make_async_copy(eg_h.at[blk, es], wgu.at[slot, :, :, pl.ds(0, F)], w_sem.at[slot, 0]),
                pltpu.make_async_copy(eu_h.at[blk, es], wgu.at[slot, :, :, pl.ds(F, F)], w_sem.at[slot, 1]),
                pltpu.make_async_copy(ed_h.at[blk, es], wd.at[slot], w_sem.at[slot, 2])]

    def w_first(blk):
        for i in range(AHEAD):
            for c in w_copies(blk, i):
                c.start()

    def w_next(blk, i):
        @pl.when(i + AHEAD < STEPS)
        def _():
            for c in w_copies(blk, i + AHEAD):
                c.start()
        for c in w_copies(blk, i):
            c.wait()
        return lax.rem(i, AHEAD + 1)

    def experts_fwd(blk, src, dst):
        def body(i, _):
            slot = w_next(blk, i)
            es = [i * Q + n for n in range(Q)]
            gus = [dot(slots[src, e], wgu[slot, n]) for n, e in enumerate(es)]
            mids = [(jax.nn.silu(gu[:, :F]) * gu[:, F:]).astype(BF16) for gu in gus]
            outs = [dot(mid, wd[slot, n]).astype(BF16) for n, mid in enumerate(mids)]
            for e, out in zip(es, outs):
                slots[dst, e] = out
            return 0
        lax.fori_loop(0, STEPS, body, 0)

    def g_copies(blk, i, slot):
        es = pl.ds(i * Q, Q)
        return [pltpu.make_async_copy(dab_v.at[slot], dab_o.at[blk, es], g_sem.at[slot, 0]),
                pltpu.make_async_copy(mid_v.at[slot], mid_o.at[blk, es], g_sem.at[slot, 1])]

    def experts_bwd(blk, zsrc, rsrc, dst):
        def body(i, _):
            slot, spare = w_next(blk, i), lax.rem(i, 2)

            @pl.when(i >= 2)
            def _():
                for c in g_copies(blk, i - 2, spare):
                    c.wait()
            es = [i * Q + n for n in range(Q)]
            gus = [dot(slots[zsrc, e], wgu[slot, n]) for n, e in enumerate(es)]
            dms = [dot_nt(slots[rsrc, e], wd[slot, n]) for n, e in enumerate(es)]
            dabs = []
            for n in range(Q):
                a, b, dm = gus[n][:, :F], gus[n][:, F:], dms[n]
                sig = jax.nn.sigmoid(a)
                act = a * sig
                mid_v[spare, n] = (act * b).astype(BF16)
                da = (dm * b * (sig * (1.0 + a * (1.0 - sig)))).astype(BF16)
                dabs.append(jnp.concatenate([da, (dm * act).astype(BF16)], axis=1))
            outs = [dot_nt(dab, wgu[slot, n]).astype(BF16) for n, dab in enumerate(dabs)]
            for n, e in enumerate(es):
                dab_v[spare, n] = dabs[n]
                slots[dst, e] = outs[n]
            for c in g_copies(blk, i, spare):
                c.start()
            return 0
        lax.fori_loop(0, STEPS, body, 0)
        for i in (STEPS - 2, STEPS - 1):
            for c in g_copies(blk, i, i % 2):
                c.wait()

    def combine(rs, ch, rt, src, gated):
        def rows_of(s):
            vals = slots[src, :, pl.ds(pl.multiple_of(s * C, C), C), :].reshape(S, D)
            want = lax.broadcasted_iota(I32, (T, 128), 0).astype(F32) + 1.0
            parts = []
            for j in range(NJ):
                val = tb[rt, s, 1, j:j + 1, :] if gated else 1.0
                parts.append(jnp.where(want == tb[rt, s, 0, j:j + 1, :], val, 0.0).astype(BF16))
            return dot(jnp.concatenate(parts, axis=1), vals)

        def sib_copy(q, n):
            return rcopy(part.at[n], sib_in.at[ch, q], sb_s.at[rs, q], sb_r.at[rs, q], dev(1))

        def body(m, _):
            first, last = 1 - lax.div(m + 6, 7), lax.div(m, 7)
            sib = lax.rem(m, 2) + first - last
            n = sib * lax.div(m + 1, 2) + (1 - sib) * (lax.div(m, 2) - 1 + last)
            q, spare = 3 - n, lax.rem(n, 2)

            @pl.when((sib == 1) & (n >= 2))
            def _():
                sib_copy(q + 2, spare).wait_send()
            part[sib * spare + (1 - sib) * 2] = rows_of(peer(2 * q + sib))

            @pl.when(sib == 1)
            def _():
                sib_copy(q, spare).start()

            @pl.when(sib == 0)
            def _():
                sib_copy(q, spare).wait_recv()
                sib_in[ch, q] += part[2]

            @pl.when(m == 2)
            def _():
                for c in tree(rs, ch):
                    c.start()

            @pl.when(m == 4)
            def _():
                fin(rs, ch, 1, 1).start()

            @pl.when(m == 6)
            def _():
                fin(rs, ch, 0, 0).start()
            return 0
        lax.fori_loop(0, 8, body, 0)
        for n in (2, 3):
            sib_copy(3 - n, n % 2).wait_send()

    def rs_mid(rs, ch):
        first, second = tree(rs, ch)
        first.wait()
        sib_in[ch, P_Y, :HALF] += tree_in[ch, LOW]
        fin(rs, ch, 1, 0).start()
        second.wait()
        sib_in[ch, P_X, HALF:] += tree_in[ch, UP]
        fin(rs, ch, 0, 1).start()

    P_OWN, P_X, P_Y, P_DIAG = range(4)

    def tree(rs, ch):
        return [rcopy(sib_in.at[ch, P_DIAG, pl.ds(h * HALF, HALF)], tree_in.at[ch, h], tr_s.at[rs, h], tr_r.at[rs, h], dev(to))
                for h, to in ((LOW, XN), (UP, YN))]

    def fin(rs, ch, axis, half):
        rows = pl.ds(half * HALF, HALF)
        return rcopy(sib_in.at[ch, P_X + axis, rows], fin_in.at[ch, axis, rows], fi_s.at[rs, axis, half], fi_r.at[rs, axis, half], dev(2 + 2 * axis))

    def rs_wait(rs, ch):
        for axis in range(2):
            for half in range(2):
                fin(rs, ch, axis, half).wait()

    def total_of(ch):
        return lambda rows: sib_in[ch, P_OWN, rows, :] + fin_in[ch, 0, rows, :] + fin_in[ch, 1, rows, :]

    def block_out(ch, h_ref, out_ref):
        total = total_of(ch)

        def body(i, _):
            rows = pl.ds(pl.multiple_of(i * ROWS, ROWS), ROWS)
            out_ref[rows, :] = (h_ref[rows, :].astype(F32) + total(rows)).astype(BF16)
            return 0
        lax.fori_loop(0, T // ROWS, body, 0)

    def save(n, slot_array, out, blk):
        return pltpu.make_async_copy(slots.at[slot_array], out.at[blk], l_sem.at[n])

    A_ZB1, A_ZF1, A_G2, A_ZB2, A_ZF2, A_G1 = range(6)
    R_B1, R_F1, R_DB2, R_F2, R_DB1 = range(5)
    w_first(LOW)
    build_tables(B1, FW1)
    pl.semaphore_wait(barrier, G)
    tables_send(B1)
    dense_fwd(LOW, xv.at[XB], hv.at[HB1], zall.at[ZB, me])
    ag_send(A_ZB1, ZB)
    build_tables(FW1, B2)
    tables_send(FW1)
    load_xf.wait()
    dense_fwd(LOW, xv.at[XF], hv.at[HF], zall.at[ZF, me])
    ag_mid(A_ZB1, ZB)
    ag_send(A_ZF1, ZF)
    build_tables(B2, FW2 + 1)
    tables_send(B2)
    tables_send(FW2)

    tables_wait(B1)
    dispatch(A_ZB1, ZB, B1, SB, False)
    save_z1 = save(0, SB, z_o, 0)
    save_z1.start()
    ag_mid(A_ZF1, ZF)
    load_g.wait()
    ag_send(A_G2, GB)
    experts_fwd(LOW, SB, RO)
    w_first(LOW)
    combine(R_B1, BB, B1, RO, True)

    tables_wait(FW1)
    dispatch(A_ZF1, ZF, FW1, SF, False)
    ag_mid(A_G2, GB)
    rs_mid(R_B1, BB)
    experts_fwd(LOW, SF, SF)
    w_first(UP)
    rs_wait(R_B1, BB)
    block_out(BB, hv.at[HB1], xv.at[XB2])
    dense_fwd(UP, xv.at[XB2], hv.at[HB2], zall.at[ZB, me])
    ag_send(A_ZB2, ZB)
    combine(R_F1, FB, FW1, SF, True)
    tables_wait(B2)
    dispatch(A_G2, GB, B2, RO, True)
    save_r2 = save(1, RO, r_o, 1)
    save_r2.start()
    ag_mid(A_ZB2, ZB)
    rs_mid(R_F1, FB)
    save_z1.wait()
    dispatch(A_ZB2, ZB, B2, SB, False)
    save_z2 = save(2, SB, z_o, 1)
    save_z2.start()
    save_r2.wait()
    experts_bwd(UP, SB, RO, RO)
    w_first(UP)
    save_z2.wait()
    load = pltpu.make_async_copy(z_o.at[LOW], slots.at[SB], l_sem.at[3])
    load.start()
    combine(R_DB2, BB, B2, RO, False)

    rs_wait(R_F1, FB)
    block_out(FB, hv.at[HF], xv.at[XF])
    dense_fwd(UP, xv.at[XF], hv.at[HF], zall.at[ZF, me])
    rs_mid(R_DB2, BB)
    ag_send(A_ZF2, ZF)
    rs_wait(R_DB2, BB)
    dense_bwd(UP, xv.at[XB2], hv.at[HB2], zall.at[GB, me], total_of(BB), zall.at[ZB, me])
    ag_mid(A_ZF2, ZF)
    ag_send(A_G1, ZB)
    tables_wait(FW2)
    dispatch(A_ZF2, ZF, FW2, SF, False)
    experts_fwd(UP, SF, SF)
    w_first(LOW)
    ag_mid(A_G1, ZB)
    combine(R_F2, FB, FW2, SF, True)

    dispatch(A_G1, ZB, B1, RO, True)
    save_r1 = save(1, RO, r_o, 0)
    save_r1.start()
    load.wait()
    rs_mid(R_F2, FB)
    experts_bwd(LOW, SB, RO, SB)
    combine(R_DB1, BB, B1, SB, False)
    rs_wait(R_F2, FB)
    block_out(FB, hv.at[HF], yv.at[LOW])
    send_y = rcopy(yv.at[LOW], y_o, o_s.at[LOW], o_r.at[LOW], stage_peer)
    send_y.start()
    rs_mid(R_DB1, BB)
    save_r1.wait()
    rs_wait(R_DB1, BB)
    dense_bwd(LOW, xv.at[XB], hv.at[HB1], zall.at[ZB, me], total_of(BB), yv.at[UP])
    send_x = rcopy(yv.at[UP], dx_o, o_s.at[UP], o_r.at[UP], stage_peer)
    send_x.start()
    send_y.wait()
    send_x.wait()


def weight_grads(z_ref, r_ref, dab_ref, mid_ref, gg_ref, gu_ref, gd_ref):
    for n in range(z_ref.shape[1]):
        dw = dot_tn(z_ref[0, n], dab_ref[0, n])
        gg_ref[0, 0, n] = dw[:, :F]
        gu_ref[0, 0, n] = dw[:, F:]
        gd_ref[0, 0, n] = dot_tn(mid_ref[0, n], r_ref[0, n])


def solution(mesh):
    def local_step(*args):
        arrays = [v[0] for v in args]
        route_fwd, gate_fwd, route_bwd, gate_bwd = arrays[8:]
        route = jnp.stack([v[blk] for blk in range(2) for v in (route_bwd, route_fwd)]).transpose(0, 2, 1)
        gate = jnp.stack([v[blk] for blk in range(2) for v in (gate_bwd, gate_fwd)]).astype(F32).transpose(0, 2, 1)
        vmem, hbm = pl.BlockSpec(memory_space=pltpu.VMEM), pl.BlockSpec(memory_space=pl.ANY)
        dma = pltpu.SemaphoreType.DMA
        tok = jax.ShapeDtypeStruct((T, D), BF16)
        wide = jax.ShapeDtypeStruct((2, E, G * C, D), BF16)
        table = (4, G, 2, 16, 128)
        scratch = [(BF16, [(3, G, T, D), (3, E, G * C, D)]), (F32, [table, table]),
                   (BF16, [(2, D, FF), (2, FF, D), (3, T, D), (3, T, D), (2, T, D)]),
                   (F32, [(3, T, D), (2, 4, T, D), (2, 2, HALF, D), (2, 2, T, D)]),
                   (BF16, [(AHEAD + 1, Q, D, 2 * F), (AHEAD + 1, Q, F, D), (2, Q, G * C, D), (2, Q, G * C, F)])]
        gather, tables, sib, tree, last = (6, 10), (4, G), (5, 4), (5, 2), (5, 2, 2)
        sems = [gather, gather, tables, tables, sib, sib, tree, tree, last, last, (AHEAD + 1, 3), (2, 2), (5,), (2,), (2,)]
        outs = pl.pallas_call(
            kernel,
            out_shape=(tok, tok, wide, wide, wide, jax.ShapeDtypeStruct((2, E, G * C, F), BF16)),
            in_specs=[hbm] * 8 + [vmem] * 2,
            out_specs=(vmem, vmem, hbm, hbm, hbm, hbm),
            scratch_shapes=[pltpu.VMEM(shape, dtype) for dtype, shapes in scratch for shape in shapes] + [dma(shape) for shape in sems],
            compiler_params=pltpu.CompilerParams(collective_id=0, has_side_effects=True, vmem_limit_bytes=67043328),
        )(*arrays[:8], route, gate)
        y_next, dx_prev, z, r, dab, mid = outs
        q = 12
        rows = [pl.BlockSpec((1, q, G * C, w), lambda b, i: (b, i, 0, 0)) for w in (D, D, D, F)]
        up = jax.ShapeDtypeStruct((1, 2, E, D, F), F32)
        down = jax.ShapeDtypeStruct((1, 2, E, F, D), F32)
        up_spec = pl.BlockSpec((1, 1, q, D, F), lambda b, i: (0, b, i, 0, 0))
        down_spec = pl.BlockSpec((1, 1, q, F, D), lambda b, i: (0, b, i, 0, 0))
        dgate, dup, ddown = pl.pallas_call(
            weight_grads,
            grid=(2, E // q),
            out_shape=(up, up, down),
            in_specs=rows,
            out_specs=(up_spec, up_spec, down_spec),
        )(z, r, dab, mid)
        return y_next[None], dx_prev[None], dgate, dup, ddown

    tok_spec = P('pp', 'ep', None)
    dense_spec = P('pp', None, None, None)
    exp_spec = P('pp', None, 'ep', None, None)
    route_spec = P('pp', None, 'ep', None)
    return jax.shard_map(local_step, mesh=mesh, in_specs=(tok_spec, tok_spec, tok_spec, dense_spec, dense_spec, exp_spec, exp_spec, exp_spec, route_spec, route_spec, route_spec, route_spec), out_specs=(tok_spec, tok_spec, exp_spec, exp_spec, exp_spec), check_vma=False)
```

time: 395 us -> 282 us (0.71)
  Pallas kernels: 353 us -> 277 us
  local copies, waits for them, and re-layouts: 37.9 us -> 3.06 us
    pallas_call x1 -> x2, Pallas kernels: 353 us -> 277 us  [the longest x1 249 us: local_step(): pl.pallas_call(kernel, out_shape=(tok, tok, wide, wide, wide, jax.ShapeDt...]
    unnamed x5 -> x6, local copies, waits for them, and re-layouts: 36.3 us -> 1.5 us
where the time goes in v2:
time: 282 us
  Pallas kernels  277 us (98%)
  local copies, waits for them, and re-layouts  3.06 us (1%)
    pallas_call x1, Pallas kernels, local_step(): pl.pallas_call(kernel, out_shape=(tok, tok, wide, wide, wide, jax.ShapeDt...  249 us
    pallas_call x1, Pallas kernels, local_step(): pl.pallas_call(weight_grads, grid=(2, E // q), out_shape=(up, up, down),...  27.5 us

profile of v2, /device:TPU:0, one launch (start us, length us, event | category | flops | bytes accessed | tf_op | source)
XLA Modules:
  0.0 281.6 jit_solution(6232764613610152254)
XLA Ops:
  0.6 0.8 slice_bitcast_fusion.6
  1.4 0.7 convert_bitcast_fusion.gt_v
  2.0 0.8 slice_bitcast_fusion.2
  2.8 0.6 add_bitcast_fusion.rt_v
  3.5 249.1 %shard_map.155 = (bf16[768,256]{1,0:T(8,128)(2,1)}, bf16[768,256]{1,0:T(8,128)(2,1)}, bf16[2,48,256,256]{3,2,1,0:T(8,128)(2,1)}, bf16[2,48,256,256]{3,2,1,0:T(8,...) custom-call(bf16[768,256]{1,0:T(8,128)(2,1)} %bitcast.37, bf16[768,256]{1,0:T(8,128)(2,1)} %bitcast.38, ...), custom_call_target="tpu_custom_call" | custom-call | tf_op jit(solution)/shard_map/pallas_call | solution.py:505
  252.6 0.0 copy-start.1
  252.6 0.0 copy-start
  252.6 27.5 %shard_map.156 = (f32[1,2,48,256,128]{4,3,2,1,0:T(8,128)}, f32[1,2,48,256,128]{4,3,2,1,0:T(8,128)}, f32[1,2,48,128,256]{4,3,2,1,0:T(8,128)}) custom-call(bf16[2,48,256,256]{3,2,1,0:T(8,128)(2,1)} %get-tuple-element.16.z_ref, bf16[2,48,256,256]{3,2,1,0:T(8,128)(2,1)} %get-tuple-element.17.r_ref, bf16[2,48,256,256]{3,2,1,0:T(8,128)(2,1)} %get-tuple-element.18.dab_ref, ...), custom_call_target="tpu_custom_call" | custom-call | tf_op jit(solution)/shard_map/pallas_call | solution.py:520
  280.1 0.0 copy-done.1
  280.1 0.7 copy.19
  280.9 0.0 copy-done
  280.9 0.7 copy.20
Async XLA Ops:
  252.6 27.5 %copy-start.1 = (bf16[768,256]{1,0:T(8,128)(2,1)S(1)}, bf16[768,256]{1,0:T(8,128)(2,1)}, u32[]{:S(2)}) copy-start(bf16[768,256]{1,0:T(8,128)(2,1)} %get-tuple-element.14) | copy-start | bytes 1179652
  252.6 28.3 %copy-start = (bf16[768,256]{1,0:T(8,128)(2,1)S(1)}, bf16[768,256]{1,0:T(8,128)(2,1)}, u32[]{:S(2)}) copy-start(bf16[768,256]{1,0:T(8,128)(2,1)} %get-tuple-element.15) | copy-start | bytes 1179652

commit v3 on v2

--- a/solution.py
+++ b/solution.py
@@ -48,7 +48,7 @@
     return a + b - 2 * a * b
 
 
-def kernel(xf_h, xb_h, gin_h, win_h, wout_h, eg_h, eu_h, ed_h, rt_v, gt_v,
+def kernel(xf_h, xb_h, gin_h, win_h, wout_h, eg_h, eu_h, ed_h, rb_v, rf_v, gb_v, gf_v,
            y_o, dx_o, z_o, r_o, dab_o, mid_o,
            zall, slots, trow, tb, w1, w2, xv, hv, yv,
            part, sib_in, tree_in, fin_in, wgu, wd, dab_v, mid_v,
@@ -80,13 +80,11 @@
     stage_peer = {"pp": 1 - pp, "ep": me}
     pl.semaphore_signal(barrier, inc=1, device_id=stage_peer, device_id_type=MESH)
 
-    pairs = [(xb_h, xv.at[XB]), (win_h, w1), (wout_h, w2), (xf_h, xv.at[XF]), (gin_h, zall.at[GB, me])]
+    pairs = [(gin_h, zall.at[GB, me]), (xb_h, xv.at[XB]), (win_h, w1), (wout_h, w2), (xf_h, xv.at[XF])]
     local = [pltpu.make_async_copy(src, dst, l_sem.at[n]) for n, (src, dst) in enumerate(pairs)]
     for c in local:
         c.start()
-    load_xb, load_w1, load_w2, load_xf, load_g = local
-    for c in (load_xb, load_w1, load_w2):
-        c.wait()
+    load_g, load_xb, load_w1, load_w2, load_xf = local
 
     def half(buf, r, h):
         return zall.at[buf, me if r is None else peer(r), pl.ds(h * HALF, HALF)]
@@ -107,8 +105,8 @@
     def ag_sib(i, buf, n):
         return ag_copy(i, PASS + n, zall.at[buf, peer((XN, YN, DIAG)[n])], SIB)
 
-    def ag_send(i, buf):
-        for c in ag_own(i, buf):
+    def ag_send(i, buf, parts=slice(None)):
+        for c in ag_own(i, buf)[parts]:
             c.start()
 
     def ag_mid(i, buf):
@@ -152,7 +150,7 @@
         sig = jax.nn.sigmoid(a)
         return sig * (1.0 + a * (1.0 - sig))
 
-    def dense_bwd(blk, x_ref, h_ref, g_ref, total, out_ref):
+    def dense_bwd(blk, x_ref, h_ref, g_ref, total, out_ref, after=None):
         def body(i, _):
             rows = pl.ds(pl.multiple_of(i * ROWS, ROWS), ROWS)
             x = x_ref[rows, :].astype(F32)
@@ -161,16 +159,21 @@
             dm = dot_nt(dh.astype(BF16), w2[blk])
             dp = (dm * silu_grad(pre)).astype(BF16)
             out_ref[rows, :] = (dh + rms_back(x, dot_nt(dp, w1[blk]))).astype(BF16)
+            if after is not None:
+                after(i, rows).start()
             return 0
         lax.fori_loop(0, T // ROWS, body, 0)
 
-    def build_tables(first, last):
-        def body(rt, _):
+    def build_tables(ch, blk):
+        rt = ch + 2 * blk
+        route_ref, gate_ref = ((rb_v, gb_v), (rf_v, gf_v))[ch]
+
+        def body(_, carry):
             acc_i = jnp.zeros((128, 128), F32)
             acc_g = jnp.zeros((128, 128), F32)
             for tc in range(T // 256):
-                rows = rt_v[rt, :, tc * 256:(tc + 1) * 256]
-                gates = gt_v[rt, :, tc * 256:(tc + 1) * 256]
+                rows = route_ref[blk, :, tc * 256:(tc + 1) * 256]
+                gates = gate_ref[blk, :, tc * 256:(tc + 1) * 256].astype(F32)
                 cols, gcols = rows.T, gates.T
                 quad = lax.shift_right_logical(rows, 7)
                 place = quad + 4 * lax.shift_right_logical(quad * 43, 9)
@@ -191,8 +194,8 @@
             trow[rt, :, 0] = acc_i.reshape(G, 16, 128)
             trow[rt, :, 1] = acc_g.reshape(G, 16, 128)
             tb[rt, me] = trow[rt, me]
-            return 0
-        lax.fori_loop(first, last, body, 0)
+            return carry
+        lax.fori_loop(0, 1, body, 0)
 
     def tables_send(rt):
         for r in range(1, G):
@@ -384,19 +387,24 @@
 
     A_ZB1, A_ZF1, A_G2, A_ZB2, A_ZF2, A_G1 = range(6)
     R_B1, R_F1, R_DB2, R_F2, R_DB1 = range(5)
-    w_first(LOW)
-    build_tables(B1, FW1)
+    build_tables(BB, LOW)
+    load_g.wait()
     pl.semaphore_wait(barrier, G)
     tables_send(B1)
+    ag_send(A_G2, GB, slice(2))
+    w_first(LOW)
+    for c in (load_xb, load_w1, load_w2):
+        c.wait()
     dense_fwd(LOW, xv.at[XB], hv.at[HB1], zall.at[ZB, me])
     ag_send(A_ZB1, ZB)
-    build_tables(FW1, B2)
+    build_tables(FB, LOW)
     tables_send(FW1)
     load_xf.wait()
     dense_fwd(LOW, xv.at[XF], hv.at[HF], zall.at[ZF, me])
     ag_mid(A_ZB1, ZB)
     ag_send(A_ZF1, ZF)
-    build_tables(B2, FW2 + 1)
+    build_tables(BB, UP)
+    build_tables(FB, UP)
     tables_send(B2)
     tables_send(FW2)
 
@@ -405,8 +413,7 @@
     save_z1 = save(0, SB, z_o, 0)
     save_z1.start()
     ag_mid(A_ZF1, ZF)
-    load_g.wait()
-    ag_send(A_G2, GB)
+    ag_send(A_G2, GB, slice(2, None))
     experts_fwd(LOW, SB, RO)
     w_first(LOW)
     combine(R_B1, BB, B1, RO, True)
@@ -421,15 +428,15 @@
     block_out(BB, hv.at[HB1], xv.at[XB2])
     dense_fwd(UP, xv.at[XB2], hv.at[HB2], zall.at[ZB, me])
     ag_send(A_ZB2, ZB)
-    combine(R_F1, FB, FW1, SF, True)
     tables_wait(B2)
     dispatch(A_G2, GB, B2, RO, True)
     save_r2 = save(1, RO, r_o, 1)
     save_r2.start()
     ag_mid(A_ZB2, ZB)
-    rs_mid(R_F1, FB)
+    combine(R_F1, FB, FW1, SF, True)
     save_z1.wait()
     dispatch(A_ZB2, ZB, B2, SB, False)
+    rs_mid(R_F1, FB)
     save_z2 = save(2, SB, z_o, 1)
     save_z2.start()
     save_r2.wait()
@@ -470,11 +477,14 @@
     rs_mid(R_DB1, BB)
     save_r1.wait()
     rs_wait(R_DB1, BB)
-    dense_bwd(LOW, xv.at[XB], hv.at[HB1], zall.at[ZB, me], total_of(BB), yv.at[UP])
-    send_x = rcopy(yv.at[UP], dx_o, o_s.at[UP], o_r.at[UP], stage_peer)
-    send_x.start()
+
+    def send_x(i, rows):
+        return rcopy(yv.at[UP, rows], dx_o.at[rows], o_s.at[1 + i], o_r.at[1 + i], stage_peer)
+
+    dense_bwd(LOW, xv.at[XB], hv.at[HB1], zall.at[ZB, me], total_of(BB), yv.at[UP], send_x)
     send_y.wait()
-    send_x.wait()
+    for i in range(T // ROWS):
+        send_x(i, pl.ds(i * ROWS, ROWS)).wait()
 
 
 def weight_grads(z_ref, r_ref, dab_ref, mid_ref, gg_ref, gu_ref, gd_ref):
@@ -489,8 +499,7 @@
     def local_step(*args):
         arrays = [v[0] for v in args]
         route_fwd, gate_fwd, route_bwd, gate_bwd = arrays[8:]
-        route = jnp.stack([v[blk] for blk in range(2) for v in (route_bwd, route_fwd)]).transpose(0, 2, 1)
-        gate = jnp.stack([v[blk] for blk in range(2) for v in (gate_bwd, gate_fwd)]).astype(F32).transpose(0, 2, 1)
+        index = [v.transpose(0, 2, 1) for v in (route_bwd, route_fwd, gate_bwd, gate_fwd)]
         vmem, hbm = pl.BlockSpec(memory_space=pltpu.VMEM), pl.BlockSpec(memory_space=pl.ANY)
         dma = pltpu.SemaphoreType.DMA
         tok = jax.ShapeDtypeStruct((T, D), BF16)
@@ -501,15 +510,15 @@
                    (F32, [(3, T, D), (2, 4, T, D), (2, 2, HALF, D), (2, 2, T, D)]),
                    (BF16, [(AHEAD + 1, Q, D, 2 * F), (AHEAD + 1, Q, F, D), (2, Q, G * C, D), (2, Q, G * C, F)])]
         gather, tables, sib, tree, last = (6, 10), (4, G), (5, 4), (5, 2), (5, 2, 2)
-        sems = [gather, gather, tables, tables, sib, sib, tree, tree, last, last, (AHEAD + 1, 3), (2, 2), (5,), (2,), (2,)]
+        sems = [gather, gather, tables, tables, sib, sib, tree, tree, last, last, (AHEAD + 1, 3), (2, 2), (5,), (4,), (4,)]
         outs = pl.pallas_call(
             kernel,
             out_shape=(tok, tok, wide, wide, wide, jax.ShapeDtypeStruct((2, E, G * C, F), BF16)),
-            in_specs=[hbm] * 8 + [vmem] * 2,
+            in_specs=[hbm] * 8 + [vmem] * 4,
             out_specs=(vmem, vmem, hbm, hbm, hbm, hbm),
             scratch_shapes=[pltpu.VMEM(shape, dtype) for dtype, shapes in scratch for shape in shapes] + [dma(shape) for shape in sems],
             compiler_params=pltpu.CompilerParams(collective_id=0, has_side_effects=True, vmem_limit_bytes=67043328),
-        )(*arrays[:8], route, gate)
+        )(*arrays[:8], *index)
         y_next, dx_prev, z, r, dab, mid = outs
         q = 12
         rows = [pl.BlockSpec((1, q, G * C, w), lambda b, i: (b, i, 0, 0)) for w in (D, D, D, F)]

time: 282 us -> 265 us (0.940)
  Pallas kernels: 277 us -> 262 us
    pallas_call x1, Pallas kernels: 249 us -> 235 us  [local_step(): pl.pallas_call(kernel, out_shape=(tok, tok, wide, wide, wide, jax.ShapeDt...]
where the time goes in v3:
time: 265 us; the launch traced here: 264 us
  Pallas kernels  262 us (99%)
    pallas_call x1, Pallas kernels, local_step(): pl.pallas_call(kernel, out_shape=(tok, tok, wide, wide, wide, jax.ShapeDt...  235 us
    pallas_call x1, Pallas kernels, local_step(): pl.pallas_call(weight_grads, grid=(2, E // q), out_shape=(up, up, down),...  27.5 us

profile of v3, /device:TPU:0, one launch (start us, length us, event | category | flops | bytes accessed | tf_op | source)
XLA Modules:
  0.0 264.3 jit_solution(6943285430648894399)
XLA Ops:
  0.6 234.6 %shard_map.155 = (bf16[768,256]{1,0:T(8,128)(2,1)}, bf16[768,256]{1,0:T(8,128)(2,1)}, bf16[2,48,256,256]{3,2,1,0:T(8,128)(2,1)}, bf16[2,48,256,256]{3,2,1,0:T(8,...) custom-call(bf16[768,256]{1,0:T(8,128)(2,1)} %bitcast.29, bf16[768,256]{1,0:T(8,128)(2,1)} %bitcast.30, ...), custom_call_target="tpu_custom_call" | custom-call | tf_op jit(solution)/shard_map/pallas_call | solution.py:514
  235.3 0.0 copy-start.1
  235.3 0.0 copy-start
  235.3 27.5 %shard_map.156 = (f32[1,2,48,256,128]{4,3,2,1,0:T(8,128)}, f32[1,2,48,256,128]{4,3,2,1,0:T(8,128)}, f32[1,2,48,128,256]{4,3,2,1,0:T(8,128)}) custom-call(bf16[2,48,256,256]{3,2,1,0:T(8,128)(2,1)} %get-tuple-element.16.z_ref, bf16[2,48,256,256]{3,2,1,0:T(8,128)(2,1)} %get-tuple-element.17.r_ref, bf16[2,48,256,256]{3,2,1,0:T(8,128)(2,1)} %get-tuple-element.18.dab_ref, ...), custom_call_target="tpu_custom_call" | custom-call | tf_op jit(solution)/shard_map/pallas_call | solution.py:529
  262.8 0.0 copy-done.1
  262.8 0.7 copy.19
  263.5 0.0 copy-done
  263.5 0.7 copy.20
Async XLA Ops:
  235.3 27.5 %copy-start.1 = (bf16[768,256]{1,0:T(8,128)(2,1)S(1)}, bf16[768,256]{1,0:T(8,128)(2,1)}, u32[]{:S(2)}) copy-start(bf16[768,256]{1,0:T(8,128)(2,1)} %get-tuple-element.14) | copy-start | bytes 1179652
  235.3 28.2 %copy-start = (bf16[768,256]{1,0:T(8,128)(2,1)S(1)}, bf16[768,256]{1,0:T(8,128)(2,1)}, u32[]{:S(2)}) copy-start(bf16[768,256]{1,0:T(8,128)(2,1)} %get-tuple-element.15) | copy-start | bytes 1179652

commit v4 on v3

--- a/solution.py
+++ b/solution.py
@@ -13,6 +13,7 @@
 S = E * C
 NJ = S // 128
 HALF = T // 2
+PIECE = HALF // 2
 ROWS = 256
 B1, FW1, B2, FW2 = range(4)
 SIB, XN, YN, DIAG = 1, 2, 4, 6
@@ -150,9 +151,14 @@
         sig = jax.nn.sigmoid(a)
         return sig * (1.0 + a * (1.0 - sig))
 
-    def dense_bwd(blk, x_ref, h_ref, g_ref, total, out_ref, after=None):
+    def dense_bwd(blk, x_ref, h_ref, g_ref, total, out_ref, before=None, after=None):
         def body(i, _):
-            rows = pl.ds(pl.multiple_of(i * ROWS, ROWS), ROWS)
+            k, h = lax.div(i, 2), lax.rem(i, 2)
+            if before is not None:
+                @pl.when(h == 0)
+                def _():
+                    before(k)
+            rows = piece(h, k)
             x = x_ref[rows, :].astype(F32)
             pre = dot(rms_norm(x).astype(BF16), w1[blk])
             dh = g_ref[rows, :].astype(F32) + rms_back(h_ref[rows, :].astype(F32), total(rows))
@@ -162,7 +168,7 @@
             if after is not None:
                 after(i, rows).start()
             return 0
-        lax.fori_loop(0, T // ROWS, body, 0)
+        lax.fori_loop(0, 4, body, 0)
 
     def build_tables(ch, blk):
         rt = ch + 2 * blk
@@ -296,7 +302,7 @@
             for c in g_copies(blk, i, i % 2):
                 c.wait()
 
-    def combine(rs, ch, rt, src, gated):
+    def combine(rs, ch, rt, src, gated, tail=False):
         def rows_of(s):
             vals = slots[src, :, pl.ds(pl.multiple_of(s * C, C), C), :].reshape(S, D)
             want = lax.broadcasted_iota(I32, (T, 128), 0).astype(F32) + 1.0
@@ -331,44 +337,52 @@
 
             @pl.when(m == 2)
             def _():
-                for c in tree(rs, ch):
-                    c.start()
-
-            @pl.when(m == 4)
-            def _():
-                fin(rs, ch, 1, 1).start()
-
-            @pl.when(m == 6)
-            def _():
-                fin(rs, ch, 0, 0).start()
+                for k in range(2):
+                    for c in tree(rs, ch, k):
+                        c.start()
+
+            if not tail:
+                for step, axis, h in ((4, 1, UP), (6, 0, LOW)):
+                    @pl.when(m == step)
+                    def _(axis=axis, h=h):
+                        for k in range(2):
+                            fin(rs, ch, axis, h, k).start()
             return 0
         lax.fori_loop(0, 8, body, 0)
         for n in (2, 3):
             sib_copy(3 - n, n % 2).wait_send()
 
-    def rs_mid(rs, ch):
-        first, second = tree(rs, ch)
-        first.wait()
-        sib_in[ch, P_Y, :HALF] += tree_in[ch, LOW]
-        fin(rs, ch, 1, 0).start()
-        second.wait()
-        sib_in[ch, P_X, HALF:] += tree_in[ch, UP]
-        fin(rs, ch, 0, 1).start()
+    def piece(h, k):
+        return pl.ds(pl.multiple_of(h * HALF + k * PIECE, PIECE), PIECE)
+
+    def rs_mid(rs, ch, tail=False):
+        for k in range(2):
+            for h, c in enumerate(tree(rs, ch, k)):
+                c.wait()
+                sib_in[ch, P_Y - h, piece(h, k)] += tree_in[ch, h, pl.ds(k * PIECE, PIECE)]
+                fin(rs, ch, 1 - h, h, k).start()
+            if tail:
+                for h in range(2):
+                    fin(rs, ch, h, h, k).start()
 
     P_OWN, P_X, P_Y, P_DIAG = range(4)
 
-    def tree(rs, ch):
-        return [rcopy(sib_in.at[ch, P_DIAG, pl.ds(h * HALF, HALF)], tree_in.at[ch, h], tr_s.at[rs, h], tr_r.at[rs, h], dev(to))
-                for h, to in ((LOW, XN), (UP, YN))]
-
-    def fin(rs, ch, axis, half):
-        rows = pl.ds(half * HALF, HALF)
-        return rcopy(sib_in.at[ch, P_X + axis, rows], fin_in.at[ch, axis, rows], fi_s.at[rs, axis, half], fi_r.at[rs, axis, half], dev(2 + 2 * axis))
+    def tree(rs, ch, k):
+        return [rcopy(sib_in.at[ch, P_DIAG, piece(h, k)], tree_in.at[ch, h, pl.ds(k * PIECE, PIECE)],
+                      tr_s.at[rs, h, k], tr_r.at[rs, h, k], dev(to)) for h, to in ((LOW, XN), (UP, YN))]
+
+    def fin(rs, ch, axis, h, k):
+        rows = piece(h, k)
+        return rcopy(sib_in.at[ch, P_X + axis, rows], fin_in.at[ch, axis, rows], fi_s.at[rs, axis, h, k], fi_r.at[rs, axis, h, k], dev(2 + 2 * axis))
+
+    def rs_piece(rs, ch, k):
+        for axis in range(2):
+            for h in range(2):
+                fin(rs, ch, axis, h, k).wait()
 
     def rs_wait(rs, ch):
-        for axis in range(2):
-            for half in range(2):
-                fin(rs, ch, axis, half).wait()
+        for k in range(2):
+            rs_piece(rs, ch, k)
 
     def total_of(ch):
         return lambda rows: sib_in[ch, P_OWN, rows, :] + fin_in[ch, 0, rows, :] + fin_in[ch, 1, rows, :]
@@ -469,25 +483,26 @@
     load.wait()
     rs_mid(R_F2, FB)
     experts_bwd(LOW, SB, RO, SB)
-    combine(R_DB1, BB, B1, SB, False)
+    combine(R_DB1, BB, B1, SB, False, True)
+    rs_mid(R_DB1, BB, True)
     rs_wait(R_F2, FB)
     block_out(FB, hv.at[HF], yv.at[LOW])
     send_y = rcopy(yv.at[LOW], y_o, o_s.at[LOW], o_r.at[LOW], stage_peer)
     send_y.start()
-    rs_mid(R_DB1, BB)
     save_r1.wait()
-    rs_wait(R_DB1, BB)
 
     def send_x(i, rows):
         return rcopy(yv.at[UP, rows], dx_o.at[rows], o_s.at[1 + i], o_r.at[1 + i], stage_peer)
 
-    dense_bwd(LOW, xv.at[XB], hv.at[HB1], zall.at[ZB, me], total_of(BB), yv.at[UP], send_x)
+    dense_bwd(LOW, xv.at[XB], hv.at[HB1], zall.at[ZB, me], total_of(BB), yv.at[UP], lambda k: rs_piece(R_DB1, BB, k), send_x)
     send_y.wait()
-    for i in range(T // ROWS):
-        send_x(i, pl.ds(i * ROWS, ROWS)).wait()
-
-
-def weight_grads(z_ref, r_ref, dab_ref, mid_ref, gg_ref, gu_ref, gd_ref):
+    for i in range(4):
+        send_x(i, piece(i % 2, i // 2)).wait()
+
+
+def weight_grads(z_ref, r_ref, dab_ref, mid_ref, y_ref, dx_ref, gg_ref, gu_ref, gd_ref, y_out, dx_out):
+    y_out[0] = y_ref[...]
+    dx_out[0] = dx_ref[...]
     for n in range(z_ref.shape[1]):
         dw = dot_tn(z_ref[0, n], dab_ref[0, n])
         gg_ref[0, 0, n] = dw[:, :F]
@@ -509,8 +524,8 @@
                    (BF16, [(2, D, FF), (2, FF, D), (3, T, D), (3, T, D), (2, T, D)]),
                    (F32, [(3, T, D), (2, 4, T, D), (2, 2, HALF, D), (2, 2, T, D)]),
                    (BF16, [(AHEAD + 1, Q, D, 2 * F), (AHEAD + 1, Q, F, D), (2, Q, G * C, D), (2, Q, G * C, F)])]
-        gather, tables, sib, tree, last = (6, 10), (4, G), (5, 4), (5, 2), (5, 2, 2)
-        sems = [gather, gather, tables, tables, sib, sib, tree, tree, last, last, (AHEAD + 1, 3), (2, 2), (5,), (4,), (4,)]
+        gather, tables, sib, tree, last = (6, 10), (4, G), (5, 4), (5, 2, 2), (5, 2, 2, 2)
+        sems = [gather, gather, tables, tables, sib, sib, tree, tree, last, last, (AHEAD + 1, 3), (2, 2), (5,), (5,), (5,)]
         outs = pl.pallas_call(
             kernel,
             out_shape=(tok, tok, wide, wide, wide, jax.ShapeDtypeStruct((2, E, G * C, F), BF16)),
@@ -520,20 +535,23 @@
             compiler_params=pltpu.CompilerParams(collective_id=0, has_side_effects=True, vmem_limit_bytes=67043328),
         )(*arrays[:8], *index)
         y_next, dx_prev, z, r, dab, mid = outs
-        q = 12
+        q = 16
         rows = [pl.BlockSpec((1, q, G * C, w), lambda b, i: (b, i, 0, 0)) for w in (D, D, D, F)]
         up = jax.ShapeDtypeStruct((1, 2, E, D, F), F32)
         down = jax.ShapeDtypeStruct((1, 2, E, F, D), F32)
         up_spec = pl.BlockSpec((1, 1, q, D, F), lambda b, i: (0, b, i, 0, 0))
         down_spec = pl.BlockSpec((1, 1, q, F, D), lambda b, i: (0, b, i, 0, 0))
-        dgate, dup, ddown = pl.pallas_call(
+        tok_in = pl.BlockSpec((T, D), lambda b, i: (0, 0))
+        tok_out = pl.BlockSpec((1, T, D), lambda b, i: (0, 0, 0))
+        tok_full = jax.ShapeDtypeStruct((1, T, D), BF16)
+        dgate, dup, ddown, y_next, dx_prev = pl.pallas_call(
             weight_grads,
             grid=(2, E // q),
-            out_shape=(up, up, down),
-            in_specs=rows,
-            out_specs=(up_spec, up_spec, down_spec),
-        )(z, r, dab, mid)
-        return y_next[None], dx_prev[None], dgate, dup, ddown
+            out_shape=(up, up, down, tok_full, tok_full),
+            in_specs=rows + [tok_in] * 2,
+            out_specs=(up_spec, up_spec, down_spec, tok_out, tok_out),
+        )(z, r, dab, mid, y_next, dx_prev)
+        return y_next, dx_prev, dgate, dup, ddown
 
     tok_spec = P('pp', 'ep', None)
     dense_spec = P('pp', None, None, None)

time: 265 us -> 259 us (0.977)
  Pallas kernels: 262 us -> 258 us
    pallas_call x1, Pallas kernels: 235 us -> 231 us  [local_step(): pl.pallas_call(kernel, out_shape=(tok, tok, wide, wide, wide, jax.ShapeDt...]
where the time goes in v4:
time: 259 us
  Pallas kernels  258 us (100%)
    pallas_call x1, Pallas kernels, local_step(): pl.pallas_call(kernel, out_shape=(tok, tok, wide, wide, wide, jax.ShapeDt...  231 us
    pallas_call x1, Pallas kernels, local_step(): pl.pallas_call(weight_grads, grid=(2, E // q), out_shape=(up, up, down, t...  27.5 us

profile of v4, /device:TPU:0, one launch (start us, length us, event | category | flops | bytes accessed | tf_op | source)
XLA Modules:
  0.0 259.0 jit_solution(6400095167598414969)
XLA Ops:
  0.6 230.9 %shard_map.155 = (bf16[768,256]{1,0:T(8,128)(2,1)}, bf16[768,256]{1,0:T(8,128)(2,1)}, bf16[2,48,256,256]{3,2,1,0:T(8,128)(2,1)}, bf16[2,48,256,256]{3,2,1,0:T(8,...) custom-call(bf16[768,256]{1,0:T(8,128)(2,1)} %bitcast.25, bf16[768,256]{1,0:T(8,128)(2,1)} %bitcast.26, ...), custom_call_target="tpu_custom_call" | custom-call | tf_op jit(solution)/shard_map/pallas_call | solution.py:529
  231.5 27.5 %shard_map.156 = (f32[1,2,48,256,128]{4,3,2,1,0:T(8,128)}, f32[1,2,48,256,128]{4,3,2,1,0:T(8,128)}, f32[1,2,48,128,256]{4,3,2,1,0:T(8,128)}, bf16[1,768,256]{2,1,0:T(8,128)(2,1)}, bf16[1,768,256]{2,1,0:T(8,128)(2,1)}) custom-call(bf16[2,48,256,256]{3,2,1,0:T(8,128)(2,1)} %get-tuple-element.16.z_ref, bf16[2,48,256,256]{3,2,1,0:T(8,128)(2,1)} %get-tuple-element.17.r_ref, ...), custom_call_target="tpu_custom_call" | custom-call | tf_op jit(solution)/shard_map/pallas_call | solution.py:547

commit v5 on v4

--- a/solution.py
+++ b/solution.py
@@ -434,8 +434,8 @@
 
     tables_wait(FW1)
     dispatch(A_ZF1, ZF, FW1, SF, False)
+    rs_mid(R_B1, BB)
     ag_mid(A_G2, GB)
-    rs_mid(R_B1, BB)
     experts_fwd(LOW, SF, SF)
     w_first(UP)
     rs_wait(R_B1, BB)

time: 259 us -> 256 us (0.988)
  Pallas kernels: 258 us -> 255 us
    pallas_call x1, Pallas kernels: 231 us -> 228 us  [local_step(): pl.pallas_call(kernel, out_shape=(tok, tok, wide, wide, wide, jax.ShapeDt...]
where the time goes in v5:
time: 256 us
  Pallas kernels  255 us (100%)
    pallas_call x1, Pallas kernels, local_step(): pl.pallas_call(kernel, out_shape=(tok, tok, wide, wide, wide, jax.ShapeDt...  228 us
    pallas_call x1, Pallas kernels, local_step(): pl.pallas_call(weight_grads, grid=(2, E // q), out_shape=(up, up, down, t...  27.5 us

profile of v5, /device:TPU:0, one launch (start us, length us, event | category | flops | bytes accessed | tf_op | source)
XLA Modules:
  0.0 255.7 jit_solution(6773986122962634815)
XLA Ops:
  0.6 227.6 %shard_map.155 = (bf16[768,256]{1,0:T(8,128)(2,1)}, bf16[768,256]{1,0:T(8,128)(2,1)}, bf16[2,48,256,256]{3,2,1,0:T(8,128)(2,1)}, bf16[2,48,256,256]{3,2,1,0:T(8,...) custom-call(bf16[768,256]{1,0:T(8,128)(2,1)} %bitcast.25, bf16[768,256]{1,0:T(8,128)(2,1)} %bitcast.26, ...), custom_call_target="tpu_custom_call" | custom-call | tf_op jit(solution)/shard_map/pallas_call | solution.py:529
  228.2 27.5 %shard_map.156 = (f32[1,2,48,256,128]{4,3,2,1,0:T(8,128)}, f32[1,2,48,256,128]{4,3,2,1,0:T(8,128)}, f32[1,2,48,128,256]{4,3,2,1,0:T(8,128)}, bf16[1,768,256]{2,1,0:T(8,128)(2,1)}, bf16[1,768,256]{2,1,0:T(8,128)(2,1)}) custom-call(bf16[2,48,256,256]{3,2,1,0:T(8,128)(2,1)} %get-tuple-element.16.z_ref, bf16[2,48,256,256]{3,2,1,0:T(8,128)(2,1)} %get-tuple-element.17.r_ref, ...), custom_call_target="tpu_custom_call" | custom-call | tf_op jit(solution)/shard_map/pallas_call | solution.py:547
